TPU v7x, 32 devices: a whole 2x2x4 slice. The times are simulated.
32 devices in a mesh: dp: 2 (over x), tp: 4 (over z), sp: 4 (over y, core).
Axes of the slice: x: 2, y: 2, z: 4, core: 2. Of those that a mesh axis runs over, the one named last changes fastest.
Arguments:
- encoded: bfloat16 [128, 512, 768], P('dp', 'sp'), parts along dimension 0
- enc_gain: float32 [768], replicated
- enc_bias: float32 [768], replicated
- probe: float32 [768], replicated
- w_query: bfloat16 [768, 12, 64], P(None, 'tp')
- b_query: float32 [12, 64], P('tp')
- w_key: bfloat16 [768, 12, 64], P(None, 'tp')
- w_value: bfloat16 [768, 12, 64], P(None, 'tp')
- b_value: float32 [12, 64], P('tp')
- w_out: bfloat16 [12, 64, 768], P('tp')
- b_out: float32 [768], replicated
- head_gain: float32 [768], replicated
- head_bias: float32 [768], replicated
- w_up: bfloat16 [768, 3072], P(None, 'tp')
- b_up: float32 [3072], P('tp')
- w_down: bfloat16 [3072, 768], P('tp')
- b_down: float32 [768], replicated
- out_grad: bfloat16 [128, 768], P('dp'), parts along dimension 0
Outputs:
- output 1: bfloat16 [128, 768], P('dp'), parts along dimension 0
- output 2: bfloat16 [128, 512, 768], P('dp', 'sp'), parts along dimension 0
- output 3: float32 [1536], P('dp'), parts along dimension 0
- output 4: float32 [1536, 12, 64], P('dp', 'tp'), parts along dimension 0
- output 5: float32 [1536, 12, 64], P('dp', 'tp'), parts along dimension 0
- output 6: float32 [1536, 12, 64], P('dp', 'tp'), parts along dimension 0
- output 7: float32 [24, 64, 768], P(('dp', 'tp')), parts along dimension 0
- output 8: float32 [1536, 3072], P('dp', 'tp'), parts along dimension 0
- output 9: float32 [6144, 768], P(('dp', 'tp')), parts along dimension 0
There are 2 independent parts. A program takes and returns all parts, laid end to end along the dimension named above; an argument that names none is the same for every part.
All inputs are finite; a program needn't handle non-finite values.
Results may differ from a plain program's by a relative error of at most 0.0186479.
Values sent between devices are 32-bit elements.
A program may use at most 1 GiB of HBM per device.

v0:
```python
import functools
import jax
import jax.numpy as jnp
from jax import lax
from jax.sharding import PartitionSpec as P

NORM_EPS = 1e-6
IN_SPECS = (P('dp', 'sp', None), P(), P(), P(), P(None, 'tp', None), P('tp', None), P(None, 'tp', None), P(None, 'tp', None), P('tp', None), P('tp', None, None), P(), P(), P(), P(None, 'tp'), P('tp'), P('tp', None), P(), P('dp', None))
OUT_SPECS = (P('dp', None), P('dp', 'sp', None), P('dp'), P('dp', 'tp', None), P('dp', 'tp', None), P('dp', 'tp', None), P(('dp', 'tp'), None, None), P('dp', 'tp'), P(('dp', 'tp'), None))


def layer_norm(rows_in, norm_gain, norm_bias):
    row_mean = jnp.mean(rows_in, axis=-1, keepdims=True)
    centred = rows_in - row_mean
    inv_std = lax.rsqrt(jnp.mean(centred * centred, axis=-1, keepdims=True) + NORM_EPS)
    return centred * inv_std * norm_gain + norm_bias


def norm_vjp(rows_in, norm_gain, norm_bias, cotangent):
    pull_back = jax.vjp(functools.partial(layer_norm, norm_gain=norm_gain, norm_bias=norm_bias), rows_in)[1]
    return pull_back(cotangent)[0]


def gelu_vjp(pre_act, cotangent):
    pull_back = jax.vjp(functools.partial(jax.nn.gelu, approximate=True), pre_act)[1]
    return pull_back(cotangent)[0]


def local_head(encoded, enc_gain, enc_bias, probe, w_query, b_query, w_key, w_value, b_value, w_out, b_out, head_gain, head_bias, w_up, b_up, w_down, b_down, out_grad):
    head_dim = b_query.shape[1]
    score_scale = head_dim ** -0.5
    enc_f32 = encoded.astype(jnp.float32)
    normed = layer_norm(enc_f32, enc_gain, enc_bias).astype(jnp.bfloat16)
    query_heads = (jnp.einsum('w,whd->hd', probe.astype(jnp.bfloat16), w_query, preferred_element_type=jnp.float32) + b_query).astype(jnp.bfloat16)
    key_heads = jnp.einsum('bnw,whd->bnhd', normed, w_key, preferred_element_type=jnp.float32).astype(jnp.bfloat16)
    value_heads = (jnp.einsum('bnw,whd->bnhd', normed, w_value, preferred_element_type=jnp.float32) + b_value).astype(jnp.bfloat16)
    scores = jnp.einsum('bnhd,hd->bhn', key_heads, query_heads, preferred_element_type=jnp.float32) * score_scale
    score_max = lax.pmax(jnp.max(scores, axis=-1, keepdims=True), 'sp')
    exp_scores = jnp.exp(scores - score_max)
    exp_total = lax.psum(jnp.sum(exp_scores, axis=-1, keepdims=True), 'sp')
    value_sum = lax.psum(jnp.einsum('bhn,bnhd->bhd', exp_scores.astype(jnp.bfloat16), value_heads, preferred_element_type=jnp.float32), 'sp')
    pooled_bf = (value_sum / exp_total).astype(jnp.bfloat16)
    attn_out = lax.psum(jnp.einsum('bhd,hdw->bw', pooled_bf, w_out, preferred_element_type=jnp.float32), 'tp') + b_out
    normed_out = layer_norm(attn_out, head_gain, head_bias).astype(jnp.bfloat16)
    pre_act = jnp.dot(normed_out, w_up, preferred_element_type=jnp.float32) + b_up
    hidden = jax.nn.gelu(pre_act, approximate=True).astype(jnp.bfloat16)
    pooled = (attn_out + lax.psum(jnp.dot(hidden, w_down, preferred_element_type=jnp.float32), 'tp') + b_down).astype(jnp.bfloat16)

    grad_w_down = jnp.einsum('bf,bw->fw', hidden, out_grad, preferred_element_type=jnp.float32)
    grad_hidden = jnp.einsum('bw,fw->bf', out_grad, w_down, preferred_element_type=jnp.float32)
    grad_pre = gelu_vjp(pre_act, grad_hidden).astype(jnp.bfloat16)
    grad_w_up = jnp.einsum('bw,bf->wf', normed_out, grad_pre, preferred_element_type=jnp.float32)
    grad_normed_out = lax.psum(jnp.einsum('bf,wf->bw', grad_pre, w_up, preferred_element_type=jnp.float32), 'tp')
    grad_attn = (out_grad.astype(jnp.float32) + norm_vjp(attn_out, head_gain, head_bias, grad_normed_out)).astype(jnp.bfloat16)
    grad_w_out = jnp.einsum('bhd,bw->hdw', pooled_bf, grad_attn, preferred_element_type=jnp.float32)
    grad_pooled = jnp.einsum('bw,hdw->bhd', grad_attn, w_out, preferred_element_type=jnp.float32).astype(jnp.bfloat16)
    weights = exp_scores / exp_total
    grad_weights = jnp.einsum('bhd,bnhd->bhn', grad_pooled, value_heads, preferred_element_type=jnp.float32)
    mean_term = lax.psum(jnp.sum(weights * grad_weights, axis=-1, keepdims=True), 'sp')
    grad_scores = (weights * (grad_weights - mean_term) * score_scale).astype(jnp.bfloat16)
    grad_query = lax.psum(jnp.einsum('bhn,bnhd->hd', grad_scores, key_heads, preferred_element_type=jnp.float32), 'sp')
    grad_keys = jnp.einsum('bhn,hd->bnhd', grad_scores, query_heads, preferred_element_type=jnp.float32).astype(jnp.bfloat16)
    grad_values = jnp.einsum('bhn,bhd->bnhd', weights.astype(jnp.bfloat16), grad_pooled, preferred_element_type=jnp.float32).astype(jnp.bfloat16)
    grad_w_key = lax.psum(jnp.einsum('bnw,bnhd->whd', normed, grad_keys, preferred_element_type=jnp.float32), 'sp')
    grad_w_value = lax.psum(jnp.einsum('bnw,bnhd->whd', normed, grad_values, preferred_element_type=jnp.float32), 'sp')
    grad_normed = lax.psum(jnp.einsum('bnhd,whd->bnw', grad_keys, w_key, preferred_element_type=jnp.float32) + jnp.einsum('bnhd,whd->bnw', grad_values, w_value, preferred_element_type=jnp.float32), 'tp')
    grad_encoded = norm_vjp(enc_f32, enc_gain, enc_bias, grad_normed).astype(jnp.bfloat16)
    grad_w_query = probe[:, None, None] * grad_query[None, :, :]
    grad_probe = lax.psum(jnp.einsum('whd,hd->w', w_query, grad_query.astype(jnp.bfloat16), preferred_element_type=jnp.float32), 'tp')
    return (pooled, grad_encoded, grad_probe, grad_w_query, grad_w_key, grad_w_value, grad_w_out, grad_w_up, grad_w_down)


def solution(mesh):
    return jax.shard_map(local_head, mesh=mesh, in_specs=IN_SPECS, out_specs=OUT_SPECS, check_vma=False)
```

profile of v0, /device:TPU:0, one launch (start us, length us, event | category | flops | bytes accessed | tf_op | source)
XLA Modules:
  0.0 1082.3 jit_solution(13580008830664704843)
XLA Ops:
  7.3 6.4 convert_reduce_fusion
  13.7 8.3 fusion.4
  23.0 9.0 fusion.39
  34.2 8.4 pmax.7
  44.0 9.1 add_convert_fusion.1
  56.6 11.8 %all-reduce = (f32[64,3,64]{0,2,1:T(8,128)S(1)}, f32[64,3]{0,1:T(4,128)S(1)}) all-reduce(f32[64,3,64]{0,2,1:T(8,128)S(1)} %bitcast.134, f32[64,3]{0,1:T(4,128)} %get-tuple-element.22), channel_id=1, replica_groups=mesh['dp'=2,'tp'=4,'sp'=4] {'sp'}, use_global_device_ids=true, to_apply=%region_4.0 | all-reduce | flops 12480 | bytes 99840 | tf_op jit(solution)/shard_map/psum | solution.py:41
  70.9 33.9 %all-reduce.8.cloned.1.call-done = f32[64,768]{1,0:T(8,128)} async-done(((f32[64,768]{1,0:T(8,128)}), f32[64,768]{1,0:T(8,128)}) %all-reduce.8.cloned.1.call-update) | async-done | bytes 196624 | tf_op jit(solution)/shard_map/psum | solution.py:43
  111.3 33.6 %all-reduce.10.cloned.1.call-done = f32[64,768]{1,0:T(8,128)} async-done(((f32[64,768]{1,0:T(8,128)}), f32[64,768]{1,0:T(8,128)}) %all-reduce.10.cloned.1.call-update) | async-done | bytes 196624 | tf_op jit(solution)/shard_map/psum | solution.py:53
  148.5 2.8 fusion.70
  152.2 5.7 psum.82
  158.7 11.2 %fusion.20 = f32[64,128,768,1]{2,1,0,3:T(8,128)} fusion(f32[3,64,128]{2,1,0:T(8,128)S(1)} %get-tuple-element.17, f32[3,64]{1,0:T(4,128)} %get-tuple-element.15, bf16[768,3,64]{0,2,1:T(8,128)(2,1)} %param.24), kind=kOutput, calls=%fused_computation.27 | convolution fusion | flops 2419064832 | bytes 25559808 | tf_op jit(solution)/shard_map/bnhd,whd->bnw/dot_general | solution.py:66
  169.9 15.7 %bitcast_add_fusion = f32[64,128,768]{2,1,0:T(8,128)} fusion(f32[64,128,768,1]{2,1,0,3:T(8,128)} %fusion.20, f32[64,3,128]{2,0,1:T(8,128)S(1)} %get-tuple-element.21, f32[64,3,64]{2,0,1:T(8,128)S(1)} %get-tuple-element.26, bf16[768,3,64]{0,2,1:T(8,128)(2,1)S(1)} %copy-done.11), kind=kOutput, calls=%fused_computation.12 | convolution fusion | flops 2425356288 | bytes 50774016 | tf_op jit(solution)/shard_map/bnhd,whd->bnw/dot_general | solution.py:66
  185.7 1.9 fusion.84
  187.6 2.0 fusion.86
  189.6 2.8 fusion.33
  192.4 7.0 psum.84
  199.6 11.7 %psum.85 = f32[768]{0:T(1024)} all-reduce(f32[768]{0:T(1024)S(1)} %convolution_reduce_fusion), channel_id=1, replica_groups=mesh['dp'=2,'tp'=4,'sp'=4] {'tp'}, use_global_device_ids=true, to_apply=%region_20.0 | all-reduce | flops 768 | bytes 6144 | tf_op jit(solution)/shard_map/psum | solution.py:69
  213.2 10.8 %fusion.47 = f32[768,3,64]{0,2,1:T(8,128)} fusion(f32[3,64,128]{2,1,0:T(8,128)S(1)} %get-tuple-element.17, f32[3,64]{1,0:T(4,128)S(1)} %copy-done.18, bf16[64,128,768]{2,1,0:T(8,128)(2,1)} %param.18, f32[768]{0:T(1024)S(1)} %copy-done.30, f32[768]{0:T(1024)S(1)} %copy-done.16, f32[64,128]{1,0:T(8,128)S(1)} %fusion.78, ...), kind=kOutput, calls=%fused_computation.43 | convolution fusion | flops 2456813568 | bytes 13343488 | tf_op jit(solution)/shard_map/bnw,bnhd->whd/dot_general | solution.py:64
  224.1 11.0 %fusion.42 = f32[768,3,64]{0,2,1:T(8,128)} fusion(f32[64,3,128]{2,0,1:T(8,128)S(1)} %get-tuple-element.21, f32[64,3,64]{2,0,1:T(8,128)S(1)} %get-tuple-element.26, bf16[64,128,768]{2,1,0:T(8,128)(2,1)} %param.18, f32[768]{0:T(1024)S(1)} %copy-done.30, f32[768]{0:T(1024)S(1)} %copy-done.16, f32[64,128]{1,0:T(8,128)S(1)} %fusion.78, ...), kind=kOutput, calls=%fused_computation.42 | convolution fusion | flops 2456813568 | bytes 13391872 | tf_op jit(solution)/shard_map/bnw,bnhd->whd/dot_general | solution.py:65
  235.1 787.5 %all-reduce.14.cloned.1.call-done = (f32[64,768]{1,0:T(8,128)}, f32[64,128,768]{2,1,0:T(8,128)}) async-done(((f32[64,768]{1,0:T(8,128)}, f32[64,128,768]{2,1,0:T(8,128)}), (f32[64,768]{1,0:T(8,128)}, f32[64,128,768]{2,1,0:T(8,128)})) %all-reduce.14.cloned.1.call-update) | async-done | bytes 25362448 | tf_op jit(solution)/shard_map/psum | solution.py:47
  1022.6 15.3 %fusion.8 = f32[64,128]{1,0:T(8,128)S(1)} fusion(bf16[64,128,768]{2,1,0:T(8,128)(2,1)} %param.18, f32[64,128,768]{2,1,0:T(8,128)} %get-tuple-element.14, f32[768]{0:T(1024)S(1)} %copy-done.16, f32[64,128]{1,0:T(8,128)S(1)} %broadcast_multiply_fusion.1), kind=kLoop, calls=%fused_computation.11 | loop fusion | flops 31449088 | bytes 37817344 | tf_op jit(solution)/shard_map/transpose(jvp())/reduce_sum | solution.py:16
  1038.0 15.9 %fusion.17 = f32[64,128]{1,0:T(8,128)S(1)} fusion(f32[64,128]{1,0:T(8,128)S(1)} %multiply_multiply_fusion.2, f32[64,128]{1,0:T(8,128)S(1)} %broadcast_multiply_fusion.1, bf16[64,128,768]{2,1,0:T(8,128)(2,1)} %param.18, f32[64,128]{1,0:T(8,128)S(1)} %fusion.78, f32[64,128,768]{2,1,0:T(8,128)} %get-tuple-element.14, f32[768]{0:T(1024)S(1)} %copy-done.16), kind=kLoop, calls=%fused_computation.22 | loop fusion | flops 50323456 | bytes 37882880 | tf_op jit(solution)/shard_map/transpose(jvp())/reduce_sum | solution.py:14
  1054.0 17.3 %add_convert_fusion = bf16[64,128,768]{2,1,0:T(8,128)(2,1)} fusion(f32[64,128]{1,0:T(8,128)S(1)} %negate_multiply_fusion, f32[64,128]{1,0:T(8,128)S(1)} %multiply_multiply_fusion.2, f32[64,128]{1,0:T(8,128)S(1)} %broadcast_multiply_fusion.1, bf16[64,128,768]{2,1,0:T(8,128)(2,1)S(1)} %bitcast.129, f32[64,128]{1,0:T(8,128)S(1)} %fusion.78, ...), kind=kLoop, calls=%fused_computation.13 | loop fusion | flops 56623104 | bytes 50465792 | tf_op jit(solution)/shard_map/convert_element_type | solution.py:67
  1071.9 1.9 copy.76
  (117 shorter events, 26.9 us)
Async XLA Ops:
  7.2 100.3 %copy-start = (bf16[768,768]{1,0:T(8,128)(2,1)S(1)}, bf16[768,768]{1,0:T(8,128)(2,1)}, u32[]{:S(2)}) copy-start(bf16[768,768]{1,0:T(8,128)(2,1)} %param.31) | copy-start | bytes 3538948
  7.2 15.7 %copy-start.16 = (f32[768]{0:T(1024)S(1)}, f32[768]{0:T(1024)}, u32[]{:S(2)}) copy-start(f32[768]{0:T(1024)} %param.19) | copy-start | bytes 9220
  7.2 15.7 %copy-start.29 = (f32[768]{0:T(1024)S(1)}, f32[768]{0:T(1024)}, u32[]{:S(2)}) copy-start(f32[768]{0:T(1024)} %param.20) | copy-start | bytes 9220
  7.3 97.5 %all-reduce.8.cloned.1.call-start = ((), (), s32[]{:S(2)}) async-start(), calls=%async_computation | async-start | bytes 393216 | tf_op jit(solution)/shard_map/psum | solution.py:43
  22.9 21.0 %copy-start.10 = (bf16[768,3,64]{0,2,1:T(8,128)(2,1)S(1)}, bf16[768,3,64]{0,2,1:T(8,128)(2,1)}, u32[]{:S(2)}) copy-start(bf16[768,3,64]{0,2,1:T(8,128)(2,1)} %param.25) | copy-start | bytes 884740
  44.0 24.6 %copy-start.5 = (bf16[3,64,768]{2,1,0:T(8,128)(2,1)S(1)}, bf16[3,64,768]{2,1,0:T(8,128)(2,1)}, u32[]{:S(2)}) copy-start(bf16[3,64,768]{2,1,0:T(8,128)(2,1)} %param.27) | copy-start | bytes 884740
  44.0 25.7 %copy-start.3 = (bf16[768,768]{1,0:T(8,128)(2,1)S(1)}, bf16[768,768]{1,0:T(8,128)(2,1)}, u32[]{:S(2)}) copy-start(bf16[768,768]{1,0:T(8,128)(2,1)} %param.33) | copy-start | bytes 3538948
  44.0 25.7 %copy-start.7 = (bf16[64,768]{1,0:T(8,128)(2,1)S(1)}, bf16[64,768]{1,0:T(8,128)(2,1)}, u32[]{:S(2)}) copy-start(bf16[64,768]{1,0:T(8,128)(2,1)} %param.35) | copy-start | bytes 294916
  44.0 60.8 %copy-start.14 = (f32[768]{0:T(1024)S(1)}, f32[768]{0:T(1024)}, u32[]{:S(2)}) copy-start(f32[768]{0:T(1024)} %param.28) | copy-start | bytes 9220
  44.0 63.5 %copy-start.15 = (f32[768]{0:T(1024)S(1)}, f32[768]{0:T(1024)}, u32[]{:S(2)}) copy-start(f32[768]{0:T(1024)} %param.29) | copy-start | bytes 9220
  68.5 38.5 %copy-start.8 = (f32[64,3,64]{0,2,1:T(8,128)}, f32[64,3,64]{0,2,1:T(8,128)S(1)}, u32[]{:S(2)}) copy-start(f32[64,3,64]{0,2,1:T(8,128)S(1)} %get-tuple-element.9) | copy-start | bytes 147460
  69.4 75.5 %all-reduce.10.cloned.1.call-start = ((), (), s32[]{:S(2)}) async-start(), calls=%async_computation.1 | async-start | bytes 393216 | tf_op jit(solution)/shard_map/psum | solution.py:53
  110.2 912.3 %all-reduce.14.cloned.1.call-start = ((), (), s32[]{:S(2)}) async-start(), calls=%async_computation.3 | async-start | bytes 50724864 | tf_op jit(solution)/shard_map/psum | solution.py:47
  185.5 25.7 %copy-start.20 = (f32[768]{0:T(1024)S(1)}, f32[768]{0:T(1024)}, u32[]{:S(2)}) copy-start(f32[768]{0:T(1024)} %param.21) | copy-start | bytes 9220
  185.5 26.6 %copy-start.9 = (f32[64,3,64]{0,2,1:T(8,128)S(1)}, f32[64,3,64]{0,2,1:T(8,128)}, u32[]{:S(2)}) copy-start(f32[64,3,64]{0,2,1:T(8,128)} %copy-done.8) | copy-start | bytes 147460
  185.6 27.7 %copy-start.18 = (f32[3,64]{1,0:T(4,128)S(1)}, f32[3,64]{1,0:T(4,128)}, u32[]{:S(2)}) copy-start(f32[3,64]{1,0:T(4,128)} %get-tuple-element.15) | copy-start | bytes 2308
  185.6 27.6 %copy-start.30 = (f32[768]{0:T(1024)S(1)}, f32[768]{0:T(1024)}, u32[]{:S(2)}) copy-start(f32[768]{0:T(1024)} %param.20) | copy-start | bytes 9220
  185.6 886.3 %all-reduce.12.cloned.1.call-start = ((), (), s32[]{:S(2)}) async-start(), calls=%async_computation.2 | async-start | bytes 2359296 | tf_op jit(solution)/shard_map/psum | solution.py:64
  1022.6 31.3 %slice-start = ((s8[12582912]{0:T(1024)(128)(4,1)}), s8[4194304]{0:T(1024)(128)(4,1)S(1)}, s32[]{:S(2)}) async-start(s8[12582912]{0:T(1024)(128)(4,1)} %bitcast.128), calls=%async_computation.4 | async-start | bytes 8388608
  1022.6 31.3 %slice-start.1 = ((s8[12582912]{0:T(1024)(128)(4,1)}), s8[4194304]{0:T(1024)(128)(4,1)S(1)}, s32[]{:S(2)}) async-start(s8[12582912]{0:T(1024)(128)(4,1)} %bitcast.128), calls=%async_computation.5 | async-start | bytes 8388608
  1037.9 16.0 %slice-start.2 = ((s8[12582912]{0:T(1024)(128)(4,1)}), s8[4194304]{0:T(1024)(128)(4,1)S(1)}, s32[]{:S(2)}) async-start(s8[12582912]{0:T(1024)(128)(4,1)} %bitcast.128), calls=%async_computation.6 | async-start | bytes 8388608
  1053.9 17.3 %copy-start.13 = (f32[64,768]{1,0:T(8,128)S(1)}, f32[64,768]{1,0:T(8,128)}, u32[]{:S(2)}) copy-start(f32[64,768]{1,0:T(8,128)} %get-tuple-element.13) | copy-start | bytes 589828
  1053.9 17.3 %copy-start.24 = (f32[768]{0:T(1024)S(1)}, f32[768]{0:T(1024)}, u32[]{:S(2)}) copy-start(f32[768]{0:T(1024)} %param.34) | copy-start | bytes 9220
  1053.9 21.8 %copy-start.1 = (bf16[768,768]{1,0:T(8,128)(2,1)S(1)}, bf16[768,768]{1,0:T(8,128)(2,1)}, u32[]{:S(2)}) copy-start(bf16[768,768]{1,0:T(8,128)(2,1)} %param.31) | copy-start | bytes 3538948
  (15 other events, 87.6 us)
Sparse Core Ops, SparseCore 0:
  69.6 35.1 all-reduce.7
  110.4 34.5 all-reduce.9
  185.7 836.7 all-reduce.13
  1025.4 36.4 all-reduce.11
where the time goes:
time: 1080 us
  waiting for transfers between devices  855 us (79%)
  matrix products  85.9 us (8%)
  other arithmetic  73.6 us (7%)
  blocking collectives  44.6 us (4%)
  between operations  14.3 us (1%)
    psum x1, waiting for transfers between devices, local_head(): lax.psum(jnp.dot(hidden, w_down, preferred_element_type=jnp.float32), 'tp')  787 us
    psum x1, waiting for transfers between devices, local_head(): lax.psum(jnp.einsum('bhd,hdw->bw', pooled_bf, w_out, preferred_element_ty...  33.9 us
    psum x1, waiting for transfers between devices, local_head(): lax.psum(jnp.einsum('bf,wf->bw', grad_pre, w_up, preferred_element_type=j...  33.6 us
  transfers between devices with their start and end apart: 4, of which 3 were waited for; matrix products, arithmetic and copies ran while one was open for 8% of the time, Pallas kernels for 0%

commit v1 on v0

v1 whole, which is shorter than its diff:
```python
import functools
import jax
import jax.numpy as jnp
from jax import lax
from jax.experimental import pallas as pl
from jax.experimental.pallas import tpu as pltpu
from jax.sharding import PartitionSpec as P

NORM_EPS = 1e-6
IN_SPECS = (P('dp', 'sp', None), P(), P(), P(), P(None, 'tp', None), P('tp', None), P(None, 'tp', None), P(None, 'tp', None), P('tp', None), P('tp', None, None), P(), P(), P(), P(None, 'tp'), P('tp'), P('tp', None), P(), P('dp', None))
OUT_SPECS = (P('dp', None), P('dp', 'sp', None), P('dp'), P('dp', 'tp', None), P('dp', 'tp', None), P('dp', 'tp', None), P(('dp', 'tp'), None, None), P('dp', 'tp'), P(('dp', 'tp'), None))
F32, BF16 = jnp.float32, jnp.bfloat16
MESH = pl.DeviceIdType.MESH
IMGS, TOK, WIDTH, HD, HEADS, TP, SP = 64, 128, 768, 64, 3, 4, 4
ROWS = IMGS * TOK
HDS = HEADS * HD
GROUP = IMGS // SP
SLOT = 8
SLOTS = TP * SLOT
QUARTER = HDS // 4
SCALE = HD ** -0.5


def dot(a, b, dims):
    return lax.dot_general(a, b, (dims, ((), ())), preferred_element_type=F32)


nn = functools.partial(dot, dims=((1,), (0,)))
nt = functools.partial(dot, dims=((1,), (1,)))
tn = functools.partial(dot, dims=((0,), (0,)))


def hi_lo(a):
    hi = a.astype(BF16).astype(F32)
    return jnp.concatenate([hi, a - hi], axis=0).astype(BF16)


def fold(a):
    half = a.shape[0] // 2
    return a[:half] + a[half:]


def row_mean(a):
    return jnp.mean(a, axis=-1, keepdims=True)


def iota(shape, axis):
    return lax.broadcasted_iota(jnp.int32, shape, axis)


def middle_kernel(x_hbm, gain_1d, bias_1d, probe_1d, wq, wk, wv, wo, bq_ref, bv_ref, bout_1d, hgain_1d, hbias_1d, bup_1d, bdown_1d, wup_hbm, wdown_hbm, og,
                  pooled_o, a_o, z_o, uc_o, c2_o, y_o, hid_o, gpre_o, ga_o, o_o, go_o, hb_o, r_o, gq_o, q_o, gp_o,
                  hx, wup, wdown, u_all, s_ref, e_ref, ml, f_ref, fo_ref, d_ref, hb, hbrx, hbg, arx, att_all, o_all,
                  gnp, gnrx, plp, plrx, pl_all, go_all, ga_all, wv_all, zl, z_ref, rrx, gprx, lsem, ssem, rsem):
    dp, t, s = lax.axis_index('dp'), lax.axis_index('tp'), lax.axis_index('sp')
    s1 = s + 1 - 2 * lax.rem(s, 2)
    s2 = lax.rem(s + 2, 4)
    s3 = lax.rem(s1 + 2, 4)
    sps = (s, s1, s2, s3)
    tps = tuple(lax.rem(t + k, 4) for k in range(4))
    mine = pl.ds(pl.multiple_of(s * GROUP, GROUP), GROUP)
    started = []
    index = iter(range(128))

    def remote(src, dst, sem, device):
        copy = pltpu.make_async_remote_copy(src_ref=src, dst_ref=dst, send_sem=ssem.at[sem], recv_sem=rsem.at[sem], device_id=device, device_id_type=MESH)
        copy.start()
        started.append(copy)
        return copy

    def to_tp(src, dst):
        return [remote(src, dst, next(index), (dp, tps[k], s)) for k in (2, 1, 3)]

    def to_sp(src, dst):
        return [remote(src, dst, next(index), (dp, t, sps[d])) for d in (3, 2, 1)]

    def arrive(copies):
        for copy in copies:
            copy.wait_recv()

    chunk = ROWS // 8
    x_copies = [pltpu.make_async_copy(x_hbm.at[pl.ds(i * chunk, chunk)], hx.at[pl.ds(i * chunk, chunk)], lsem.at[i]) for i in range(8)]
    x_copies += [pltpu.make_async_copy(wup_hbm, wup, lsem.at[8]), pltpu.make_async_copy(wdown_hbm, wdown, lsem.at[9])]
    for copy in x_copies:
        copy.start()

    o_all[...] = jnp.zeros_like(o_all)
    go_all[...] = jnp.zeros_like(go_all)
    gprx[...] = jnp.zeros_like(gprx)
    barrier = pltpu.get_barrier_semaphore()
    peers = [(dp, tps[k], sps[d]) for k in range(4) for d in range(4) if (k, d) != (0, 0)]
    peers += [(1 - dp, t, s), (1 - dp, t, s1)]
    for peer in peers:
        pl.semaphore_signal(barrier, inc=1, device_id=peer, device_id_type=MESH)

    gain, bias, probe, bout, hgain, hbias, bup, bdown = [v[...].reshape(1, WIDTH) for v in (gain_1d, bias_1d, probe_1d, bout_1d, hgain_1d, hbias_1d, bup_1d, bdown_1d)]
    bq, bv = [jnp.concatenate([v[h:h + 1] for h in range(HEADS)], axis=1) for v in (bq_ref, bv_ref)]
    probe_rows = jnp.broadcast_to(probe, (16, WIDTH)).astype(BF16)
    query = (nt(probe_rows, wq[...]) + bq).astype(BF16).astype(F32)
    diag = iota((SLOT, HDS), 0) == iota((SLOT, HDS), 1) // HD
    query_diag = jnp.where(diag, query[:SLOT], 0.0)
    u_all[t] = fold(nn(hi_lo(query_diag), wk[...]))
    wv_all[t] = wv[...].astype(F32)
    q_o[...] = jnp.zeros_like(q_o)
    gq_o[...] = jnp.zeros_like(gq_o)
    q_o[:, 0:HDS] = query[:SLOT]

    pl.semaphore_wait(barrier, len(peers))
    u_copies = to_tp(u_all.at[t], u_all.at[t])
    part = lax.rem(s, 2) + 2 * dp
    part_rows = pl.ds(pl.multiple_of(part * QUARTER, 16), QUARTER)
    wv_copies = to_tp(wv_all.at[t, part_rows], wv_all.at[t, part_rows])

    step_rows = 256
    gain_row, bias_row = gain, bias

    def norm_step(i):
        rows = pl.ds(pl.multiple_of(i * step_rows, step_rows), step_rows)
        x = hx[rows].astype(F32)
        centred = x - row_mean(x)
        inv = lax.rsqrt(row_mean(centred * centred) + NORM_EPS)
        hx[rows] = (centred * inv * gain_row + bias_row).astype(BF16)

    for c in range(8):
        x_copies[c].wait()
        pl.loop(c * chunk // step_rows, (c + 1) * chunk // step_rows)(norm_step)

    arrive(u_copies)
    u = u_all[...].reshape(SLOTS, WIDTH)
    u_split = hi_lo(u)
    lane = iota((SLOTS, TOK), 1)
    wide = 512

    def score_step(i, carry):
        m_all, l_all = carry
        rows = pl.ds(pl.multiple_of(i * wide, wide), wide)
        raw = fold(nt(u_split, hx[rows]))
        s_ref[:, :, rows] = raw.reshape(TP, SLOT, wide)
        for j in range(wide // TOK):
            score = raw[:, j * TOK:(j + 1) * TOK] * SCALE
            top = jnp.max(score, axis=1, keepdims=True)
            e = jnp.exp(score - top)
            total = jnp.sum(e, axis=1, keepdims=True)
            e_ref[:, :, pl.ds(pl.multiple_of(i * wide + j * TOK, TOK), TOK)] = e.reshape(TP, SLOT, TOK)
            here = lane == i * (wide // TOK) + j
            m_all = jnp.where(here, top, m_all)
            l_all = jnp.where(here, total, l_all)
        return m_all, l_all

    m_own, l_own = lax.fori_loop(0, ROWS // wide, score_step, (jnp.zeros((SLOTS, TOK), F32), jnp.ones((SLOTS, TOK), F32)))
    ml[s, 0:SLOTS] = m_own
    ml[s, SLOTS:] = l_own
    ml_copies = to_sp(ml.at[s], ml.at[s])

    def pooled_step(b, row_base):
        image = row_base + b
        e_own = e_ref[t, :, pl.ds(pl.multiple_of(image * TOK, TOK), TOK)]
        result = fold(nn(hi_lo(e_own), hx[pl.ds(pl.multiple_of(image * TOK, TOK), TOK)]))
        for h in range(HEADS):
            hb[h, pl.ds(image, 1), :] = result[h:h + 1]

    hb_copies = []
    for d in (3, 2, 1, 0):
        base = pl.multiple_of(sps[d] * GROUP, GROUP)
        pl.loop(0, GROUP, unroll=4)(functools.partial(pooled_step, row_base=base))
        if d == 3:
            arrive(ml_copies)
            tops = [ml[k, 0:SLOTS] for k in range(SP)]
            top = functools.reduce(jnp.maximum, tops)
            total = sum(ml[k, SLOTS:] * jnp.exp(tops[k] - top) for k in range(SP))
            f_ref[...] = (jnp.exp(m_own - top) / total).reshape(TP, SLOT, TOK)
            fo_ref[...] = f_ref[t].T
        group = pl.ds(base, GROUP)
        for h in range(HEADS):
            hb[h, group, :] = hb[h, group, :] * fo_ref[group, h:h + 1]
        if d:
            hb_copies.append(remote(hb.at[:, group], hbrx.at[s], next(index), (dp, t, sps[d])))

    arrive(wv_copies)
    forward_copies = []
    for k in (2, 1, 3):
        block = wv_all.at[tps[(4 - k) % 4], part_rows]
        for device in ((dp, t, s1), (1 - dp, t, s), (1 - dp, t, s1)):
            forward_copies.append(remote(block, block, next(index), device))

    arrive(hb_copies)
    lane_head = iota((GROUP, HDS), 1) // HD
    o = jnp.zeros((GROUP, HDS), F32)
    for h in range(HEADS):
        hsum = hb[h, mine, :] + hbrx[s1, h] + hbrx[s2, h] + hbrx[s3, h]
        hbg[h, mine, :] = hsum
        o = jnp.where(lane_head == h, fold(nt(hi_lo(hsum), wv[...])), o)
    o_plain = o
    o = o + bv
    o_all[mine, 0:HDS] = o
    arx[t] = nn(o.astype(BF16), wo[...])
    att_copies = to_tp(arx.at[t], arx.at[t])
    x_copies[8].wait()
    x_copies[9].wait()
    grad_hidden = nt(og[...], wdown[...])
    arrive(att_copies)
    att_all[mine, :] = arx[0] + arx[1] + arx[2] + arx[3] + bout
    att_copies = to_sp(att_all.at[mine], att_all.at[mine])
    o_copies = to_sp(o_all.at[mine], o_all.at[mine])
    arrive(att_copies)

    att = att_all[...]
    centred = att - row_mean(att)
    inv = lax.rsqrt(row_mean(centred * centred) + NORM_EPS)
    y = (centred * inv * hgain + hbias).astype(BF16)
    y_o[...] = y
    pre = nn(y, wup[...]) + bup
    square = pre * pre
    tanh = jnp.tanh((2 / jnp.pi) ** 0.5 * (pre + 0.044715 * (square * pre)))
    hid = (0.5 * pre * (1.0 + tanh)).astype(BF16)
    slope = 0.5 * (1.0 + tanh) + 0.5 * pre * (1.0 - tanh * tanh) * ((2 / jnp.pi) ** 0.5 * (1.0 + 3 * 0.044715 * square))
    gpre = (grad_hidden * slope).astype(BF16)
    gpre_o[...] = gpre
    hid_o[...] = hid
    gnp[...] = nt(gpre, wup[...])
    gnrx[t] = gnp[mine, :]
    gn_copies = to_tp(gnrx.at[t], gnrx.at[t])
    plp[...] = nn(hid, wdown[...])
    plrx[t] = plp[mine, :]
    pl_copies = to_tp(plrx.at[t], plrx.at[t])
    arrive(gn_copies)
    grad_y = (gnrx[0] + gnrx[1] + gnrx[2] + gnrx[3]) * hgain
    att16 = att_all[mine, :]
    centred = att16 - row_mean(att16)
    inv = lax.rsqrt(row_mean(centred * centred) + NORM_EPS)
    unit = centred * inv
    grad_att = og[mine, :].astype(F32) + inv * (grad_y - row_mean(grad_y) - unit * row_mean(grad_y * unit))
    go = nt(grad_att.astype(BF16), wo[...]).astype(BF16).astype(F32)
    tail_lane = iota((GROUP, HD), 1)
    tail = jnp.zeros((GROUP, HD), F32)
    for h in range(HEADS):
        delta = jnp.sum(jnp.where(lane_head == h, go * o_plain, 0.0), axis=1, keepdims=True)
        tail = jnp.where(tail_lane == h, delta, tail)
    go_all[t, mine, 0:HDS] = go
    go_all[t, mine, HDS:] = tail
    go_copies = to_tp(go_all.at[t, mine], go_all.at[t, mine])
    ga_all[mine, :] = grad_att
    arrive(go_copies)
    go_copies = to_sp(go_all.at[:, mine], go_all.at[:, mine])
    ga_copies = to_sp(ga_all.at[mine], ga_all.at[mine])
    arrive(pl_copies)
    pl_all[mine, :] = plrx[0] + plrx[1] + plrx[2] + plrx[3] + att16 + bdown
    pl_copies = to_sp(pl_all.at[mine], pl_all.at[mine])
    hbg_copies = to_sp(hbg.at[:, mine], hbg.at[:, mine])
    bias_u = jnp.sum(u * bias_row, axis=1, keepdims=True)
    gain_u = u * gain_row
    uc_o[...] = (gain_u - row_mean(gain_u)).astype(BF16)
    arrive(go_copies)
    arrive(forward_copies)

    zmask = jnp.where(iota((SLOT, HDS), 0) == iota((SLOT, HDS), 1) // HD, 1.0, 0.0)
    for k in range(TP):
        def spread(b, k=k):
            zl[k, pl.ds(pl.multiple_of(b * SLOT, SLOT), SLOT), :] = go_all[k, pl.ds(b, 1), 0:HDS] * zmask
        pl.loop(0, IMGS, unroll=8)(spread)
        d_ref[k] = jnp.concatenate([go_all[k, :, TOK:], jnp.zeros((IMGS, TOK), F32)], axis=0).T[HD:HD + SLOT]
        wv_k = wv_all[k].astype(BF16)

        def z_step(i, k=k, wv_k=wv_k):
            rows = pl.ds(pl.multiple_of(i * 128, 128), 128)
            z_ref[k, rows, :] = nn(zl[k, rows, :].astype(BF16), wv_k)
        pl.loop(0, IMGS * SLOT // 128)(z_step)

    f_all = f_ref[...].reshape(SLOTS, TOK)
    d_all = d_ref[...].reshape(SLOTS, TOK)

    def back_step(b):
        lanes = pl.ds(pl.multiple_of(b * TOK, TOK), TOK)
        eight = pl.ds(pl.multiple_of(b * SLOT, SLOT), SLOT)
        z = jnp.concatenate([z_ref[k, eight, :] for k in range(TP)], axis=0)
        grad_p = fold(nt(hi_lo(z), hx[lanes]))
        bias_z = jnp.sum(z * bias_row, axis=1, keepdims=True)
        gain_z = z * gain_row
        z_o[b] = (gain_z - row_mean(gain_z)).astype(BF16)
        here = lane == b
        f_col = jnp.sum(jnp.where(here, f_all, 0.0), axis=1, keepdims=True)
        d_col = jnp.sum(jnp.where(here, d_all, 0.0), axis=1, keepdims=True)
        p = e_ref[:, :, lanes].reshape(SLOTS, TOK) * f_col
        ds = p * (grad_p - d_col) * SCALE
        raw = s_ref[:, :, lanes].reshape(SLOTS, TOK)
        terms = ds * (raw - bias_u) + p * (grad_p - bias_z)
        c2_o[pl.ds(b, 1), :] = jnp.sum(terms, axis=0, keepdims=True) * (1.0 / WIDTH)
        a_o[b] = jnp.concatenate([ds, p], axis=0).astype(BF16)
        e_ref[:, :, lanes] = ds.reshape(TP, SLOT, TOK)

    pl.loop(0, IMGS, unroll=2)(back_step)

    def r_step(i, acc):
        rows = pl.ds(pl.multiple_of(i * chunk, chunk), chunk)
        return acc + nn(hi_lo(e_ref[t, :, rows]), hx[rows])

    r_part = fold(lax.fori_loop(0, 8, r_step, jnp.zeros((2 * SLOT, WIDTH), F32)))
    rrx[s] = r_part
    r_copies = to_sp(rrx.at[s], rrx.at[s])

    def query_grad(r_rows):
        return jnp.sum(jnp.where(diag, fold(nt(hi_lo(r_rows), wk[...])), 0.0), axis=0, keepdims=True)

    gq_part = jnp.where(iota((SLOT, HDS), 0) == 0, query_grad(r_part), 0.0)
    gp_part = fold(nn(hi_lo(gq_part), wq[...]))
    slot = t * SP + s
    for i in range(WIDTH // TOK):
        gprx[slot, i:i + 1, :] = gp_part[0:1, i * TOK:(i + 1) * TOK]
    gp_copies = [remote(gprx.at[slot], gprx.at[slot], next(index), (dp, tps[k], sps[d])) for k in (2, 1, 3, 0) for d in (3, 2, 1, 0) if (k, d) != (0, 0)]

    arrive(pl_copies)
    pooled_o[...] = pl_all[...].astype(BF16)
    arrive(ga_copies)
    ga_o[...] = ga_all[...].astype(BF16)
    arrive(o_copies)
    o_o[...] = o_all[...].astype(BF16)
    go_o[...] = go_all[t].astype(BF16)
    arrive(hbg_copies)
    hb_o[...] = hbg[...].astype(BF16)
    arrive(r_copies)
    r_sum = rrx[0] + rrx[1] + rrx[2] + rrx[3]
    r_o[...] = r_sum
    gq_o[:, 0:HDS] = jnp.broadcast_to(query_grad(r_sum), (SLOT, HDS))
    arrive(gp_copies)
    gp_o[...] = sum(gprx[i] for i in range(TP * SP))
    for copy in started:
        copy.wait_send()


N_MESSAGES = 96


def middle(*args):
    vm, sds = pltpu.VMEM, jax.ShapeDtypeStruct
    outs = (sds((IMGS, WIDTH), BF16), sds((IMGS, 2 * SLOTS, TOK), BF16), sds((IMGS, SLOTS, WIDTH), BF16), sds((SLOTS, WIDTH), BF16), sds((IMGS, TOK), F32),
            sds((IMGS, WIDTH), BF16), sds((IMGS, WIDTH), BF16), sds((IMGS, WIDTH), BF16), sds((IMGS, WIDTH), BF16), sds((IMGS, 256), BF16), sds((IMGS, 256), BF16),
            sds((HEADS, IMGS, WIDTH), BF16), sds((SLOT, WIDTH), F32), sds((SLOT, 256), F32), sds((SLOT, 256), F32), sds((SLOT, TOK), F32))
    scratch = [vm((ROWS, WIDTH), BF16), vm((WIDTH, WIDTH), BF16), vm((WIDTH, WIDTH), BF16), vm((TP, SLOT, WIDTH), F32),
               vm((TP, SLOT, ROWS), F32), vm((TP, SLOT, ROWS), F32), vm((SP, 2 * SLOTS, TOK), F32), vm((TP, SLOT, TOK), F32), vm((TOK, SLOT), F32), vm((TP, SLOT, TOK), F32),
               vm((HEADS, IMGS, WIDTH), F32), vm((SP, HEADS, GROUP, WIDTH), F32), vm((HEADS, IMGS, WIDTH), F32),
               vm((TP, GROUP, WIDTH), F32), vm((IMGS, WIDTH), F32), vm((IMGS, 256), F32),
               vm((IMGS, WIDTH), F32), vm((TP, GROUP, WIDTH), F32), vm((IMGS, WIDTH), F32), vm((TP, GROUP, WIDTH), F32), vm((IMGS, WIDTH), F32),
               vm((TP, IMGS, 256), F32), vm((IMGS, WIDTH), F32), vm((TP, HDS, WIDTH), F32), vm((TP, IMGS * SLOT, HDS), F32), vm((TP, IMGS * SLOT, WIDTH), F32),
               vm((SP, SLOT, WIDTH), F32), vm((TP * SP, SLOT, TOK), F32),
               pltpu.SemaphoreType.DMA((10,)), pltpu.SemaphoreType.DMA((N_MESSAGES,)), pltpu.SemaphoreType.DMA((N_MESSAGES,))]
    any_spec, vm_spec = pl.BlockSpec(memory_space=pl.ANY), pl.BlockSpec(memory_space=vm)
    in_specs = [any_spec] + [vm_spec] * 14 + [any_spec] * 2 + [vm_spec]
    return pl.pallas_call(middle_kernel, out_shape=outs, in_specs=in_specs, out_specs=[vm_spec] * len(outs), scratch_shapes=scratch,
                          compiler_params=pltpu.CompilerParams(collective_id=0, has_side_effects=True, vmem_limit_bytes=60 * 1024 * 1024), name='middle')(*args)


STEPS = 8


def final_kernel(x_ref, a_ref, z_ref, uc_ref, c2_ref, y_ref, gpre_ref, hid_ref, og_ref, o_ref, ga_ref, go_ref, hb_ref, gq_ref, q_ref, r_ref, probe_ref, gp_ref, pool_ref,
                 gx_ref, gup_ref, gdown_ref, gout_ref, gvalue_ref, gquery_ref, gkey_ref, gprobe_ref, pooled_ref):
    step = pl.program_id(0)
    images = IMGS // STEPS
    c2_cols = jnp.concatenate([c2_ref[...]] * (TOK // images), axis=0).T
    for b in range(images):
        rows = slice(b * TOK, (b + 1) * TOK)
        mixed = tn(a_ref[b], jnp.concatenate([uc_ref[...], z_ref[b]], axis=0))
        x = x_ref[rows].astype(F32)
        centred = x - row_mean(x)
        inv = lax.rsqrt(row_mean(centred * centred) + NORM_EPS)
        gx_ref[rows] = (inv * mixed - centred * (inv * inv * c2_cols[:, b:b + 1])).astype(BF16)

    @pl.when(step < WIDTH // TOK)
    def _():
        gup_ref[...] = tn(y_ref[...], gpre_ref[...])
        gdown_ref[...] = tn(hid_ref[...], og_ref[...])

    @pl.when(step == 6)
    def _():
        gout_ref[...] = tn(o_ref[...], ga_ref[...])[:HDS]

    @pl.when(step == 5)
    def _():
        gquery_ref[...] = gq_ref[...].T[:HDS, 0:1] * probe_ref[...].reshape(1, WIDTH)
        query = q_ref[...].T
        for h in range(HEADS):
            gkey_ref[h * HD:(h + 1) * HD] = query[h * HD:(h + 1) * HD, 0:1] * r_ref[h:h + 1]
        for i in range(WIDTH // TOK):
            gprobe_ref[i * TOK:(i + 1) * TOK] = gp_ref[i]
        pooled_ref[...] = pool_ref[...]

    @pl.when(step == 7)
    def _():
        go = go_ref[...]
        for h in range(HEADS):
            gvalue_ref[h * HD:(h + 1) * HD] = tn(go, hb_ref[h])[h * HD:(h + 1) * HD]


def final(*args):
    sds = jax.ShapeDtypeStruct
    images = IMGS // STEPS
    last = WIDTH // TOK - 1

    def whole(shape):
        return pl.BlockSpec(shape, lambda i: (0,) * len(shape))

    cols = pl.BlockSpec((IMGS, TOK), lambda i: (0, jnp.minimum(i, last)))
    out_rows = pl.BlockSpec((TOK, WIDTH), lambda i: (jnp.minimum(i, last), 0))
    x_spec = pl.BlockSpec((images * TOK, WIDTH), lambda i: (i, 0))
    in_specs = [x_spec, pl.BlockSpec((images, 2 * SLOTS, TOK), lambda i: (i, 0, 0)), pl.BlockSpec((images, SLOTS, WIDTH), lambda i: (i, 0, 0)),
                whole((SLOTS, WIDTH)), pl.BlockSpec((images, TOK), lambda i: (i, 0)), cols, whole((IMGS, WIDTH)), cols, whole((IMGS, WIDTH)),
                whole((IMGS, 256)), whole((IMGS, WIDTH)), whole((IMGS, 256)), whole((HEADS, IMGS, WIDTH)),
                whole((SLOT, 256)), whole((SLOT, 256)), whole((SLOT, WIDTH)), whole((WIDTH,)), whole((SLOT, TOK)), whole((IMGS, WIDTH))]
    outs = (sds((ROWS, WIDTH), BF16), sds((WIDTH, WIDTH), F32), sds((WIDTH, WIDTH), F32), sds((HDS, WIDTH), F32), sds((HDS, WIDTH), F32), sds((HDS, WIDTH), F32), sds((HDS, WIDTH), F32), sds((WIDTH,), F32), sds((IMGS, WIDTH), BF16))
    out_specs = [x_spec, out_rows, out_rows] + [whole((HDS, WIDTH))] * 4 + [whole((WIDTH,)), whole((IMGS, WIDTH))]
    return pl.pallas_call(final_kernel, grid=(STEPS,), out_shape=outs, in_specs=in_specs, out_specs=out_specs,
                          compiler_params=pltpu.CompilerParams(dimension_semantics=('arbitrary',), vmem_limit_bytes=63 * 1024 * 1024), name='final')(*args)


def local_head(encoded, enc_gain, enc_bias, probe, w_query, b_query, w_key, w_value, b_value, w_out, b_out, head_gain, head_bias, w_up, b_up, w_down, b_down, out_grad):
    def flat(w):
        return jnp.transpose(w, (1, 2, 0)).reshape(HDS, WIDTH)

    def unflat(g):
        return jnp.transpose(g.reshape(HEADS, HD, WIDTH), (2, 0, 1))

    x = encoded.reshape(ROWS, WIDTH)
    pool, a, z, uc, c2, y, hid, gpre, ga, o, go, hb, r, gq, q, gp = middle(
        x, enc_gain, enc_bias, probe, flat(w_query), flat(w_key), flat(w_value), w_out.reshape(HDS, WIDTH), b_query, b_value,
        b_out, head_gain, head_bias, b_up, b_down, w_up, w_down, out_grad)
    grad_x, grad_w_up, grad_w_down, grad_w_out, grad_w_value, grad_w_query, grad_w_key, grad_probe, pooled = final(
        x, a, z, uc, c2, y, gpre, hid, out_grad, o, ga, go, hb, gq, q, r, probe, gp, pool)
    return (pooled, grad_x.reshape(IMGS, TOK, WIDTH), grad_probe, unflat(grad_w_query), unflat(grad_w_key), unflat(grad_w_value),
            grad_w_out.reshape(HEADS, HD, WIDTH), grad_w_up, grad_w_down)


def solution(mesh):
    return jax.shard_map(local_head, mesh=mesh, in_specs=IN_SPECS, out_specs=OUT_SPECS, check_vma=False)
```

time: 1080 us -> 116 us (0.11)
  waiting for transfers between devices: 855 us -> 0 us
  Pallas kernels: 0 us -> 115 us
  matrix products: 85.9 us -> 0 us
  other arithmetic: 73.6 us -> 0 us
  blocking collectives: 44.6 us -> 0 us
  between operations: 14.3 us -> 0.66 us
    psum x4 -> x0, waiting for transfers between devices: 855 us -> none  [the longest x1 787 us: local_head(): lax.psum(jnp.dot(hidden, w_down, preferred_element_type=jnp.float32), 'tp')]
    pallas_call x0 -> x2, Pallas kernels: none -> 115 us  [the longest x1 91.4 us: middle(): pl.pallas_call(middle_kernel, out_shape=outs, in_specs=in_specs, out_spec...]
    dot_general x21 -> x0, matrix products: 85.9 us -> none  [the longest x1 15.7 us: local_head(): jnp.einsum('bnhd,whd->bnw', grad_values, w_value, preferred_element_type=...]
    reduce_sum x10 -> x0, other arithmetic: 52.3 us -> none  [the longest x2 17.2 us: layer_norm(): centred = rows_in - row_mean]
    psum x4 -> x0, blocking collectives: 36.2 us -> none  [the longest x1 11.8 us: local_head(): lax.psum(jnp.einsum('bhn,bnhd->bhd', exp_scores.astype(jnp.bfloat16), val...]
    convert_element_type x5 -> x0, other arithmetic: 18 us -> none  [the longest x1 17.3 us: local_head(): norm_vjp(enc_f32, enc_gain, enc_bias, grad_normed).astype(jnp.bfloat16)]
  transfers between devices with their start and end apart: 4 -> 0, of which waited for: 3 -> 0; matrix products, arithmetic and copies ran while one was open for 8% -> 0% of each run, Pallas kernels for 0% -> 0%
where the time goes in v1:
time: 116 us
  Pallas kernels  115 us (99%)
    pallas_call x1, Pallas kernels, middle(): pl.pallas_call(middle_kernel, out_shape=outs, in_specs=in_specs, out_spec...  91.4 us
    pallas_call x1, Pallas kernels, final(): pl.pallas_call(final_kernel, grid=(STEPS,), out_shape=outs, in_specs=in_s...  23.6 us

profile of v1, /device:TPU:0, one launch (start us, length us, event | category | flops | bytes accessed | tf_op | source)
XLA Modules:
  0.0 115.7 jit_solution(12266606200096719096)
XLA Ops:
  0.6 91.4 %middle.1 = (bf16[64,768]{1,0:T(8,128)(2,1)}, bf16[64,64,128]{2,1,0:T(8,128)(2,1)}, bf16[64,32,768]{2,1,0:T(8,128)(2,1)}, bf16[32,768]{1,0:T(8,128)(2,1)}, f32[6...) custom-call(bf16[8192,768]{1,0:T(8,128)(2,1)} %bitcast.22, ...), custom_call_target="tpu_custom_call" | custom-call | tf_op jit(solution)/shard_map/middle/pallas_call | solution.py:348
  92.0 23.6 %final.1 = (bf16[8192,768]{1,0:T(8,128)(2,1)}, f32[768,768]{1,0:T(8,128)}, f32[768,768]{1,0:T(8,128)}, f32[192,768]{1,0:T(8,128)}, f32[192,768]{1,0:T(8,128)}, /...) custom-call(bf16[8192,768]{1,0:T(8,128)(2,1)} %bitcast.23, ...), custom_call_target="tpu_custom_call" | custom-call | tf_op jit(solution)/shard_map/final/pallas_call | solution.py:411

commit v2 on v1

v2 whole, which is shorter than its diff:
```python
import functools
import jax
import jax.numpy as jnp
from jax import lax
from jax.experimental import pallas as pl
from jax.experimental.pallas import tpu as pltpu
from jax.sharding import PartitionSpec as P

NORM_EPS = 1e-6
IN_SPECS = (P('dp', 'sp', None), P(), P(), P(), P(None, 'tp', None), P('tp', None), P(None, 'tp', None), P(None, 'tp', None), P('tp', None), P('tp', None, None), P(), P(), P(), P(None, 'tp'), P('tp'), P('tp', None), P(), P('dp', None))
OUT_SPECS = (P('dp', None), P('dp', 'sp', None), P('dp'), P('dp', 'tp', None), P('dp', 'tp', None), P('dp', 'tp', None), P(('dp', 'tp'), None, None), P('dp', 'tp'), P(('dp', 'tp'), None))
F32, BF16 = jnp.float32, jnp.bfloat16
MESH = pl.DeviceIdType.MESH
IMGS, TOK, WIDTH, HD, HEADS, TP, SP = 64, 128, 768, 64, 3, 4, 4
ROWS = IMGS * TOK
HDS = HEADS * HD
GROUP = IMGS // SP
SLOT = 8
PAIRS = TP // 2
SLOTS = PAIRS * SLOT
QUARTER = HDS // 4
SCALE = HD ** -0.5


def dot(a, b, dims):
    return lax.dot_general(a, b, (dims, ((), ())), preferred_element_type=F32)


nn = functools.partial(dot, dims=((1,), (0,)))
nt = functools.partial(dot, dims=((1,), (1,)))
tn = functools.partial(dot, dims=((0,), (0,)))


def hi_lo(a):
    hi = a.astype(BF16).astype(F32)
    return jnp.concatenate([hi, a - hi], axis=0).astype(BF16)


def fold(a):
    half = a.shape[0] // 2
    return a[:half] + a[half:]


def row_mean(a):
    return jnp.mean(a, axis=-1, keepdims=True)


def iota(shape, axis):
    return lax.broadcasted_iota(jnp.int32, shape, axis)


def middle_kernel(x_hbm, gain_1d, bias_1d, probe_1d, wq, wk, wv, wo, bq_ref, bv_ref, bout_1d, hgain_1d, hbias_1d, bup_1d, bdown_1d, wup_hbm, wdown_hbm, og,
                  pooled_o, small_o, xh_o, a_o, z_o, uc_o, coef_o, y_o, hid_o, gpre_o, ga_o, o_o, go_o, hb_o,
                  hx, wup, wdown, u_rx, s_ref, e_ref, inv_ref, ml, f_ref, w_ref, d_ref, hb, hbrx, hbg, arx, att_all, o_all,
                  gnp, gnrx, plp, plrx, pl_all, ga_all, wv_all, go_all, zl, z_ref, a_s, z_s, uc_s, coef_s, y_s, hid_s, gpre_s, ga_s, hb_s, r_acc, rrx, gprx, lsem, ssem, rsem):
    dp, t, s = lax.axis_index('dp'), lax.axis_index('tp'), lax.axis_index('sp')
    s1 = s + 1 - 2 * lax.rem(s, 2)
    s2 = lax.rem(s + 2, 4)
    s3 = lax.rem(s1 + 2, 4)
    sps = (s, s1, s2, s3)
    tps = tuple(lax.rem(t + k, 4) for k in range(4))
    pair, odd = t // 2, lax.rem(t, 2)
    mine = pl.ds(pl.multiple_of(s * GROUP, GROUP), GROUP)
    started = []
    index = iter(range(N_MESSAGES))

    def remote(src, dst, device):
        sem = next(index)
        copy = pltpu.make_async_remote_copy(src_ref=src, dst_ref=dst, send_sem=ssem.at[sem], recv_sem=rsem.at[sem], device_id=device, device_id_type=MESH)
        copy.start()
        started.append(copy)
        return copy

    def to_tp(src, dst):
        return [remote(src, dst, (dp, tps[k], s)) for k in (2, 1, 3)]

    def to_sp(src, dst):
        return [remote(src, dst, (dp, t, sps[d])) for d in (3, 2, 1)]

    def arrive(copies):
        for copy in copies:
            copy.wait_recv()

    puts = []

    def put(src, dst):
        puts.append(pltpu.make_async_copy(src, dst, lsem.at[6 + len(puts)]))
        puts[-1].start()

    def own(rows):
        return jnp.where(odd == 1, pltpu.roll(rows, SLOT // 2, 0), rows)

    order = (3, 2, 1, 0)
    span = GROUP * TOK
    bases = [pl.multiple_of(sps[d] * span, span) for d in order]
    x_copies = [pltpu.make_async_copy(x_hbm.at[pl.ds(base, span)], hx.at[pl.ds(base, span)], lsem.at[i]) for i, base in enumerate(bases)]
    x_copies += [pltpu.make_async_copy(wup_hbm, wup, lsem.at[4]), pltpu.make_async_copy(wdown_hbm, wdown, lsem.at[5])]
    for copy in x_copies:
        copy.start()

    o_all[...] = jnp.zeros_like(o_all)
    go_all[...] = jnp.zeros_like(go_all)
    gprx[...] = jnp.zeros_like(gprx)
    barrier = pltpu.get_barrier_semaphore()
    peers = [(dp, tps[k], sps[d]) for k in range(4) for d in range(4) if (k, d) != (0, 0)]
    peers += [(1 - dp, t, s)]
    for peer in peers:
        pl.semaphore_signal(barrier, inc=1, device_id=peer, device_id_type=MESH)

    gain, bias, probe, bout, hgain, hbias, bup, bdown = [v[...].reshape(1, WIDTH) for v in (gain_1d, bias_1d, probe_1d, bout_1d, hgain_1d, hbias_1d, bup_1d, bdown_1d)]
    bq, bv = [jnp.concatenate([v[h:h + 1] for h in range(HEADS)], axis=1) for v in (bq_ref, bv_ref)]
    probe_rows = jnp.broadcast_to(probe, (16, WIDTH)).astype(BF16)
    query = (nt(probe_rows, wq[...]) + bq).astype(BF16).astype(F32)[:SLOT]
    slot_row, slot_lane = iota((SLOT, HDS), 0), iota((SLOT, HDS), 1) // HD

    def slots_of(parity):
        return (slot_row // 4 == parity) & (lax.rem(slot_row, 4) == slot_lane)

    diag = slots_of(0)
    u_rx[t] = fold(nn(hi_lo(jnp.where(slots_of(odd), query, 0.0)), wk[...]))
    wv_all[t] = wv[...].astype(F32)
    head_shift = fold(nt(hi_lo(jnp.broadcast_to(bias, (SLOT, WIDTH))), wv[...]))[0:1] + bv

    step_rows = 2 * TOK
    image_lane = iota((TOK, TOK), 1)

    def norm_step(i, base):
        rows = pl.ds(pl.multiple_of(base + i * step_rows, step_rows), step_rows)
        x = hx[rows].astype(F32)
        centred = x - row_mean(x)
        inv = lax.rsqrt(row_mean(centred * centred) + NORM_EPS)
        hx[rows] = (centred * inv).astype(BF16)
        image = base // TOK + 2 * i
        inv_ref[...] = jnp.where(image_lane == image, inv[:TOK], jnp.where(image_lane == image + 1, inv[TOK:], inv_ref[...]))

    def norm_group(i):
        x_copies[i].wait()
        pl.loop(0, span // step_rows)(functools.partial(norm_step, base=bases[i]))
        block = pl.ds(bases[i], span)
        put(hx.at[block], xh_o.at[block])

    norm_group(0)
    norm_group(1)
    pl.semaphore_wait(barrier, len(peers))
    u_copies = to_tp(u_rx.at[t], u_rx.at[t])
    quarters = [pl.ds(pl.multiple_of((lax.rem(s, 2) + 2 * x) * QUARTER, 16), QUARTER) for x in (dp, 1 - dp)]
    norm_group(2)
    norm_group(3)

    def relay_x(whole, copies):
        arrive(copies)
        blocks = [whole.at[tps[(4 - k) % 4], quarters[0]] for k in (2, 1, 3)]
        across = [remote(b, b, (1 - dp, t, s)) for b in blocks]
        return across, [remote(b, b, (dp, t, s1)) for b in blocks]

    def relay_core(whole, across):
        arrive(across)
        blocks = [whole.at[tps[(4 - k) % 4], quarters[1]] for k in (2, 1, 3)]
        return [remote(b, b, (dp, t, s1)) for b in blocks]

    arrive(u_copies)
    wv_copies = to_tp(wv_all.at[t, quarters[0]], wv_all.at[t, quarters[0]])
    u = jnp.concatenate([(u_rx[2 * k] + u_rx[2 * k + 1]) * gain for k in range(PAIRS)], axis=0)
    u_split = hi_lo(u)
    uc_s[...] = (u - row_mean(u)).astype(BF16)
    put(uc_s, uc_o)
    lane = iota((SLOTS, TOK), 1)
    wide = 4 * TOK

    def score_step(i, carry, base):
        m_all, l_all = carry
        start = pl.multiple_of(base + i * wide, wide)
        raw = fold(nt(u_split, hx[pl.ds(start, wide)]))
        s_ref[:, :, pl.ds(start, wide)] = raw.reshape(PAIRS, SLOT, wide)
        for j in range(wide // TOK):
            score = raw[:, j * TOK:(j + 1) * TOK] * SCALE
            top = jnp.max(score, axis=1, keepdims=True)
            e = jnp.exp(score - top)
            total = jnp.sum(e, axis=1, keepdims=True)
            e_ref[:, :, pl.ds(pl.multiple_of(start + j * TOK, TOK), TOK)] = e.reshape(PAIRS, SLOT, TOK)
            here = lane == i * (wide // TOK) + j
            m_all = jnp.where(here, top, m_all)
            l_all = jnp.where(here, total, l_all)
        return m_all, l_all

    def pooled_step(i, base):
        lanes = pl.ds(pl.multiple_of(base + i * TOK, TOK), TOK)
        result = fold(nn(hi_lo(own(e_ref[pair, :, lanes])), hx[lanes]))
        for h in range(HEADS):
            hb[h, pl.ds(base // TOK + i, 1), :] = result[h:h + 1]

    ml_copies, hb_copies = [], []
    for d, base in zip(order, bases):
        m_own, l_own = lax.fori_loop(0, span // wide, functools.partial(score_step, base=base), (jnp.zeros((SLOTS, TOK), F32), jnp.ones((SLOTS, TOK), F32)))
        ml[s, sps[d], 0:SLOTS] = m_own
        ml[s, sps[d], SLOTS:] = l_own
        ml_copies.append(to_sp(ml.at[s, sps[d]], ml.at[s, sps[d]]))
        pl.loop(0, GROUP, unroll=4)(functools.partial(pooled_step, base=base))
        group = pl.ds(pl.multiple_of(sps[d] * GROUP, GROUP), GROUP)
        if d:
            hb_copies.append(remote(hb.at[:, group], hbrx.at[s], (dp, t, sps[d])))
        else:
            hbrx[s] = hb[:, group, :]


    def weights_of(g, sources):
        tops = [ml[k, g, 0:SLOTS] for k in range(SP)]
        top = functools.reduce(jnp.maximum, tops)
        total = sum(ml[k, g, SLOTS:] * jnp.exp(tops[k] - top) for k in range(SP))
        return [jnp.exp(ml[k, g, 0:SLOTS] - top) / total for k in sources]

    for i, d in enumerate((3, 2, 1)):
        ml_copies[i][i].wait_recv()
    cols = []
    for k, weight in enumerate(weights_of(s, range(SP))):
        w_ref[k] = weight.reshape(PAIRS, SLOT, TOK)
        cols.append(own(w_ref[k, pair]).T)
    arrive(hb_copies)
    lane_head = iota((GROUP, HDS), 1) // HD
    o_part = jnp.zeros((GROUP, HDS), F32)
    for h in range(HEADS):
        hsum = sum(hbrx[k, h] * cols[k][0:GROUP, h:h + 1] for k in range(SP)) * gain
        hbg[h, mine, :] = hsum + bias
        o_part = jnp.where(lane_head == h, fold(nt(hi_lo(hsum), wv[...])), o_part)
    o_all[mine, 0:HDS] = o_part + head_shift
    arx[t] = nn((o_part + head_shift).astype(BF16), wo[...])
    att_copies = to_tp(arx.at[t], arx.at[t])
    wv_across, wv_core = relay_x(wv_all, wv_copies)
    x_copies[4].wait()
    x_copies[5].wait()
    grad_hidden = nt(og[...], wdown[...])
    for i, d in enumerate((3, 2, 1)):
        arrive([c for j, c in enumerate(ml_copies[i]) if j != i])
    arrive(ml_copies[3])
    for g in range(SP):
        f_ref[g] = weights_of(g, [s])[0]
    inv_ref[...] = inv_ref[...].T
    arrive(att_copies)
    att_all[mine, :] = arx[0] + arx[1] + arx[2] + arx[3] + bout
    att_copies = to_sp(att_all.at[mine], att_all.at[mine])
    o_copies = to_sp(o_all.at[mine], o_all.at[mine])
    arrive(att_copies)

    att = att_all[...]
    centred = att - row_mean(att)
    inv = lax.rsqrt(row_mean(centred * centred) + NORM_EPS)
    y = (centred * inv * hgain + hbias).astype(BF16)
    pre = nn(y, wup[...]) + bup
    square = pre * pre
    tanh = jnp.tanh((2 / jnp.pi) ** 0.5 * (pre + 0.044715 * (square * pre)))
    slope = 0.5 * (1.0 + tanh) + 0.5 * pre * (1.0 - tanh * tanh) * ((2 / jnp.pi) ** 0.5 * (1.0 + 3 * 0.044715 * square))
    gpre = (grad_hidden * slope).astype(BF16)
    gnp[...] = nt(gpre, wup[...])
    gnrx[t] = gnp[mine, :]
    gn_copies = to_tp(gnrx.at[t], gnrx.at[t])
    hid = (0.5 * pre * (1.0 + tanh)).astype(BF16)
    for value, kept, out in ((y, y_s, y_o), (gpre, gpre_s, gpre_o), (hid, hid_s, hid_o)):
        kept[...] = value
        put(kept, out)
    plp[...] = nn(hid, wdown[...])
    plrx[t] = plp[mine, :]
    wv_second = relay_core(wv_all, wv_across)
    arrive(gn_copies)
    grad_y = (gnrx[0] + gnrx[1] + gnrx[2] + gnrx[3]) * hgain
    att16 = att_all[mine, :]
    centred = att16 - row_mean(att16)
    inv = lax.rsqrt(row_mean(centred * centred) + NORM_EPS)
    unit = centred * inv
    grad_att = og[mine, :].astype(F32) + inv * (grad_y - row_mean(grad_y) - unit * row_mean(grad_y * unit))
    go = nt(grad_att.astype(BF16), wo[...]).astype(BF16).astype(F32)
    tail_lane = iota((GROUP, HD), 1)
    tail = jnp.zeros((GROUP, HD), F32)
    for h in range(HEADS):
        delta = jnp.sum(jnp.where(lane_head == h, go * o_part, 0.0), axis=1, keepdims=True)
        tail = jnp.where(tail_lane == h, delta, tail)
    go_all[t, mine, 0:HDS] = go
    go_all[t, mine, HDS:] = tail
    go_copies = to_tp(go_all.at[t, mine], go_all.at[t, mine])
    ga_all[mine, :] = grad_att
    arrive(go_copies)
    go_copies = to_sp(go_all.at[:, mine], go_all.at[:, mine])
    pl_copies = to_tp(plrx.at[t], plrx.at[t])
    arrive(wv_core)
    arrive(wv_second)
    arrive(go_copies)
    ga_copies = to_sp(ga_all.at[mine], ga_all.at[mine])
    hbg_copies = to_sp(hbg.at[:, mine], hbg.at[:, mine])

    for j in range(PAIRS):
        deltas = [jnp.concatenate([go_all[2 * j + k, :, TOK:], jnp.zeros((IMGS, TOK), F32)], axis=0).T[HD:HD + SLOT // 2] for k in range(2)]
        d_ref[j] = jnp.concatenate(deltas, axis=0)
    for k in range(TP):
        mask = jnp.where(slots_of(k % 2), 1.0, 0.0)

        def spread(b, k=k, mask=mask):
            zl[k, pl.ds(pl.multiple_of(b * SLOT, SLOT), SLOT), :] = go_all[k, pl.ds(b, 1), 0:HDS] * mask
        pl.loop(0, IMGS, unroll=8)(spread)
    for j in range(PAIRS):
        wv_pair = [wv_all[k].astype(BF16) for k in (2 * j, 2 * j + 1)]

        def z_step(i, j=j, wv_pair=wv_pair):
            rows = pl.ds(pl.multiple_of(i * 128, 128), 128)
            z_ref[j, rows, :] = sum(nn(zl[2 * j + k, rows, :].astype(BF16), wv_pair[k]) for k in range(2)) * gain
        pl.loop(0, IMGS * SLOT // 128)(z_step)

    d_all = d_ref[...].reshape(SLOTS, TOK)
    r_acc[...] = jnp.zeros_like(r_acc)

    batch = 4

    def back_step(i):
        images = [i * batch + j for j in range(batch)]
        rows = pl.ds(pl.multiple_of(i * batch * TOK, batch * TOK), batch * TOK)
        x = hx[rows]
        grads = []
        for j, b in enumerate(images):
            eight = pl.ds(pl.multiple_of(b * SLOT, SLOT), SLOT)
            z = jnp.concatenate([z_ref[k, eight, :] for k in range(PAIRS)], axis=0)
            grads.append(fold(nt(hi_lo(z), x[j * TOK:(j + 1) * TOK])))
            z_s[b] = (z - row_mean(z)).astype(BF16)
        all_ds = []
        for b, grad_p in zip(images, grads):
            lanes = pl.ds(pl.multiple_of(b * TOK, TOK), TOK)
            f_col = jnp.sum(jnp.where(lane == lax.rem(b, GROUP), f_ref[b // GROUP], 0.0), axis=1, keepdims=True)
            d_col = jnp.sum(jnp.where(lane == b, d_all, 0.0), axis=1, keepdims=True)
            p = e_ref[:, :, lanes].reshape(SLOTS, TOK) * f_col
            ds = p * (grad_p - d_col) * SCALE
            raw = s_ref[:, :, lanes].reshape(SLOTS, TOK)
            inv_row = inv_ref[pl.ds(b, 1), :]
            coef_s[pl.ds(b, 1), :] = jnp.sum(ds * raw + p * grad_p, axis=0, keepdims=True) * inv_row * (-1.0 / WIDTH)
            a_s[b] = (jnp.concatenate([ds, p], axis=0) * inv_row).astype(BF16)
            all_ds.append(own(jnp.where(pair == 1, ds[SLOT:], ds[:SLOT])))
        r_acc[...] += nn(hi_lo(jnp.concatenate(all_ds, axis=1)), x)

    for g in range(SP):
        pl.loop(g * GROUP // batch, (g + 1) * GROUP // batch)(back_step)
        group = pl.ds(g * GROUP, GROUP)
        put(a_s.at[group], a_o.at[group])
        put(z_s.at[group], z_o.at[group])
        if g == 0:
            arrive(pl_copies)
            pl_all[mine, :] = plrx[0] + plrx[1] + plrx[2] + plrx[3] + att_all[mine, :] + bdown
            pl_copies = to_sp(pl_all.at[mine], pl_all.at[mine])
            put(go_all.at[t], go_o)
        if g == 2:
            arrive(o_copies)
            put(o_all, o_o)
            arrive(ga_copies)
            ga_s[...] = ga_all[...].astype(BF16)
            put(ga_s, ga_o)
    put(coef_s, coef_o)

    r_part = fold(r_acc[...]) * gain
    rrx[s] = r_part
    r_copies = to_sp(rrx.at[s], rrx.at[s])

    def query_grad(r_rows):
        return jnp.sum(jnp.where(diag, fold(nt(hi_lo(r_rows), wk[...])), 0.0), axis=0, keepdims=True)

    gq_part = jnp.where(iota((SLOT, HDS), 0) == 0, query_grad(r_part), 0.0)
    gp_part = fold(nn(hi_lo(gq_part), wq[...]))
    slot = t * SP + s
    for i in range(WIDTH // TOK):
        gprx[slot, i:i + 1, :] = gp_part[0:1, i * TOK:(i + 1) * TOK]
    gp_copies = [remote(gprx.at[slot], gprx.at[slot], (dp, tps[k], sps[d])) for k in (2, 1, 3, 0) for d in (3, 2, 1, 0) if (k, d) != (0, 0)]

    arrive(pl_copies)
    pooled_o[...] = pl_all[...].astype(BF16)
    arrive(hbg_copies)
    hb_s[...] = hbg[...].astype(BF16)
    put(hb_s, hb_o)
    arrive(r_copies)
    r_sum = rrx[0] + rrx[1] + rrx[2] + rrx[3]
    small_o[...] = r_sum
    small_o[3:4, :] = jnp.zeros((1, WIDTH), F32)
    small_o[4:5, :] = jnp.zeros((1, WIDTH), F32)
    small_o[3:4, 0:HDS] = query_grad(r_sum)
    small_o[4:5, 0:HDS] = query[0:1]
    arrive(gp_copies)
    gp = sum(gprx[i] for i in range(TP * SP))
    for i in range(WIDTH // TOK):
        small_o[5:6, i * TOK:(i + 1) * TOK] = gp[i:i + 1]
    for copy in started:
        copy.wait_send()
    for copy in puts:
        copy.wait()


N_MESSAGES = 112


def middle(*args):
    vm, sds = pltpu.VMEM, jax.ShapeDtypeStruct
    wide = sds((IMGS, WIDTH), BF16)
    outs = (wide, sds((SLOT, WIDTH), F32), sds((ROWS, WIDTH), BF16), sds((IMGS, 2 * SLOTS, TOK), BF16), sds((IMGS, SLOTS, WIDTH), BF16), sds((SLOTS, WIDTH), BF16), sds((IMGS, TOK), F32),
            wide, wide, wide, wide, sds((IMGS, 256), F32), sds((IMGS, 256), F32), sds((HEADS, IMGS, WIDTH), BF16))
    scratch = [vm((ROWS, WIDTH), BF16), vm((WIDTH, WIDTH), BF16), vm((WIDTH, WIDTH), BF16), vm((TP, SLOT, WIDTH), F32),
               vm((PAIRS, SLOT, ROWS), F32), vm((PAIRS, SLOT, ROWS), F32), vm((TOK, TOK), F32), vm((SP, SP, 2 * SLOTS, TOK), F32), vm((SP, SLOTS, TOK), F32), vm((SP, PAIRS, SLOT, TOK), F32), vm((PAIRS, SLOT, TOK), F32),
               vm((HEADS, IMGS, WIDTH), F32), vm((SP, HEADS, GROUP, WIDTH), F32), vm((HEADS, IMGS, WIDTH), F32),
               vm((TP, GROUP, WIDTH), F32), vm((IMGS, WIDTH), F32), vm((IMGS, 256), F32),
               vm((IMGS, WIDTH), F32), vm((TP, GROUP, WIDTH), F32), vm((IMGS, WIDTH), F32), vm((TP, GROUP, WIDTH), F32), vm((IMGS, WIDTH), F32),
               vm((IMGS, WIDTH), F32), vm((TP, HDS, WIDTH), F32), vm((TP, IMGS, 256), F32), vm((TP, IMGS * SLOT, HDS), F32), vm((PAIRS, IMGS * SLOT, WIDTH), F32),
               vm((IMGS, 2 * SLOTS, TOK), BF16), vm((IMGS, SLOTS, WIDTH), BF16), vm((SLOTS, WIDTH), BF16), vm((IMGS, TOK), F32),
               vm((IMGS, WIDTH), BF16), vm((IMGS, WIDTH), BF16), vm((IMGS, WIDTH), BF16), vm((IMGS, WIDTH), BF16), vm((HEADS, IMGS, WIDTH), BF16), vm((2 * SLOT, WIDTH), F32),
               vm((SP, SLOT, WIDTH), F32), vm((TP * SP, SLOT, TOK), F32),
               pltpu.SemaphoreType.DMA((32,)), pltpu.SemaphoreType.DMA((N_MESSAGES,)), pltpu.SemaphoreType.DMA((N_MESSAGES,))]
    any_spec, vm_spec = pl.BlockSpec(memory_space=pl.ANY), pl.BlockSpec(memory_space=vm)
    in_specs = [any_spec] + [vm_spec] * 14 + [any_spec] * 2 + [vm_spec]
    out_specs = [vm_spec] * 2 + [any_spec] * (len(outs) - 2)
    return pl.pallas_call(middle_kernel, out_shape=outs, in_specs=in_specs, out_specs=out_specs, scratch_shapes=scratch,
                          compiler_params=pltpu.CompilerParams(collective_id=0, has_side_effects=True, vmem_limit_bytes=63 * 1024 * 1024), name='middle')(*args)


STEPS = 8


def final_kernel(xh_ref, a_ref, z_ref, uc_ref, coef_ref, y_ref, gpre_ref, hid_ref, og_ref, o_ref, ga_ref, go_ref, hb_ref, small_ref, probe_ref, pool_ref,
                 gx_ref, gup_ref, gdown_ref, gout_ref, gvalue_ref, gquery_ref, gkey_ref, gprobe_ref, pooled_ref):
    step = pl.program_id(0)
    images = IMGS // STEPS
    cols = jnp.concatenate([coef_ref[...]] * (TOK // images), axis=0).T
    for b in range(images):
        rows = slice(b * TOK, (b + 1) * TOK)
        mixed = tn(a_ref[b], jnp.concatenate([uc_ref[...], z_ref[b]], axis=0))
        gx_ref[rows] = (mixed + xh_ref[rows].astype(F32) * cols[:, b:b + 1]).astype(BF16)

    @pl.when(step < WIDTH // TOK)
    def _():
        gup_ref[...] = tn(y_ref[...], gpre_ref[...])
        gdown_ref[...] = tn(hid_ref[...], og_ref[...])

    @pl.when(step == 6)
    def _():
        gout_ref[...] = tn(o_ref[...].astype(BF16), ga_ref[...])[:HDS]

    @pl.when(step == 5)
    def _():
        turned = jnp.concatenate([small_ref[...], jnp.zeros((TOK - SLOT, WIDTH), F32)], axis=0)[:, :256].T
        gquery_ref[...] = turned[:HDS, 3:4] * probe_ref[...].reshape(1, WIDTH)
        for h in range(HEADS):
            gkey_ref[h * HD:(h + 1) * HD] = turned[h * HD:(h + 1) * HD, 4:5] * small_ref[h:h + 1]
        gprobe_ref[...] = small_ref[5]
        pooled_ref[...] = pool_ref[...]

    @pl.when(step == 7)
    def _():
        go = go_ref[...].astype(BF16)
        for h in range(HEADS):
            gvalue_ref[h * HD:(h + 1) * HD] = tn(go, hb_ref[h])[h * HD:(h + 1) * HD]


def final(*args):
    sds = jax.ShapeDtypeStruct
    images = IMGS // STEPS
    last = WIDTH // TOK - 1

    def whole(shape):
        return pl.BlockSpec(shape, lambda i: (0,) * len(shape))

    cols = pl.BlockSpec((IMGS, TOK), lambda i: (0, jnp.minimum(i, last)))
    out_rows = pl.BlockSpec((TOK, WIDTH), lambda i: (jnp.minimum(i, last), 0))
    x_spec = pl.BlockSpec((images * TOK, WIDTH), lambda i: (i, 0))
    in_specs = [x_spec, pl.BlockSpec((images, 2 * SLOTS, TOK), lambda i: (i, 0, 0)), pl.BlockSpec((images, SLOTS, WIDTH), lambda i: (i, 0, 0)),
                whole((SLOTS, WIDTH)), pl.BlockSpec((images, TOK), lambda i: (i, 0)), cols, whole((IMGS, WIDTH)), cols, whole((IMGS, WIDTH)),
                whole((IMGS, 256)), whole((IMGS, WIDTH)), whole((IMGS, 256)), whole((HEADS, IMGS, WIDTH)),
                whole((SLOT, WIDTH)), whole((WIDTH,)), whole((IMGS, WIDTH))]
    outs = (sds((ROWS, WIDTH), BF16), sds((WIDTH, WIDTH), F32), sds((WIDTH, WIDTH), F32), sds((HDS, WIDTH), F32), sds((HDS, WIDTH), F32), sds((HDS, WIDTH), F32), sds((HDS, WIDTH), F32), sds((WIDTH,), F32), sds((IMGS, WIDTH), BF16))
    out_specs = [x_spec, out_rows, out_rows] + [whole((HDS, WIDTH))] * 4 + [whole((WIDTH,)), whole((IMGS, WIDTH))]
    return pl.pallas_call(final_kernel, grid=(STEPS,), out_shape=outs, in_specs=in_specs, out_specs=out_specs,
                          compiler_params=pltpu.CompilerParams(dimension_semantics=('arbitrary',), vmem_limit_bytes=63 * 1024 * 1024), name='final')(*args)


def local_head(encoded, enc_gain, enc_bias, probe, w_query, b_query, w_key, w_value, b_value, w_out, b_out, head_gain, head_bias, w_up, b_up, w_down, b_down, out_grad):
    def flat(w):
        return jnp.transpose(w, (1, 2, 0)).reshape(HDS, WIDTH)

    def unflat(g):
        return jnp.transpose(g.reshape(HEADS, HD, WIDTH), (2, 0, 1))

    x = encoded.reshape(ROWS, WIDTH)
    pool, small, xh, a, z, uc, coef, y, hid, gpre, ga, o, go, hb = middle(
        x, enc_gain, enc_bias, probe, flat(w_query), flat(w_key), flat(w_value), w_out.reshape(HDS, WIDTH), b_query, b_value,
        b_out, head_gain, head_bias, b_up, b_down, w_up, w_down, out_grad)
    grad_x, grad_w_up, grad_w_down, grad_w_out, grad_w_value, grad_w_query, grad_w_key, grad_probe, pooled = final(
        xh, a, z, uc, coef, y, gpre, hid, out_grad, o, ga, go, hb, small, probe, pool)
    return (pooled, grad_x.reshape(IMGS, TOK, WIDTH), grad_probe, unflat(grad_w_query), unflat(grad_w_key), unflat(grad_w_value),
            grad_w_out.reshape(HEADS, HD, WIDTH), grad_w_up, grad_w_down)


def solution(mesh):
    return jax.shard_map(local_head, mesh=mesh, in_specs=IN_SPECS, out_specs=OUT_SPECS, check_vma=False)
```

time: 116 us -> 91.6 us (0.79)
  Pallas kernels: 115 us -> 90.7 us
    pallas_call x1, Pallas kernels: 91.4 us -> 73.3 us  [middle(): pl.pallas_call(middle_kernel, out_shape=outs, in_specs=in_specs, out_spec...]
    pallas_call x1, Pallas kernels: 23.6 us -> 17.4 us  [final(): pl.pallas_call(final_kernel, grid=(STEPS,), out_shape=outs, in_specs=in_s...]
where the time goes in v2:
time: 91.6 us; the launch traced here: 91.4 us
  Pallas kernels  90.7 us (99%)
    pallas_call x1, Pallas kernels, middle(): pl.pallas_call(middle_kernel, out_shape=outs, in_specs=in_specs, out_spec...  73.3 us
    pallas_call x1, Pallas kernels, final(): pl.pallas_call(final_kernel, grid=(STEPS,), out_shape=outs, in_specs=in_s...  17.4 us

profile of v2, /device:TPU:0, one launch (start us, length us, event | category | flops | bytes accessed | tf_op | source)
XLA Modules:
  0.0 91.4 jit_solution(10355231096108353239)
XLA Ops:
  0.6 73.3 %middle.1 = (bf16[64,768]{1,0:T(8,128)(2,1)}, f32[8,768]{1,0:T(8,128)}, bf16[8192,768]{1,0:T(8,128)(2,1)}, bf16[64,32,128]{2,1,0:T(8,128)(2,1)}, bf16[64,16,768]...) custom-call(bf16[8192,768]{1,0:T(8,128)(2,1)} %bitcast.22, ...), custom_call_target="tpu_custom_call" | custom-call | tf_op jit(solution)/shard_map/middle/pallas_call | solution.py:410
  73.9 17.4 %final.1 = (bf16[8192,768]{1,0:T(8,128)(2,1)}, f32[768,768]{1,0:T(8,128)}, f32[768,768]{1,0:T(8,128)}, f32[192,768]{1,0:T(8,128)}, f32[192,768]{1,0:T(8,128)}, /...) custom-call(bf16[8192,768]{1,0:T(8,128)(2,1)} %get-tuple-element.32.xh_ref, ...), custom_call_target="tpu_custom_call" | custom-call | tf_op jit(solution)/shard_map/final/pallas_call | solution.py:469

commit v3 on v2

v3 whole, which is shorter than its diff:
```python
import functools
import jax
import jax.numpy as jnp
from jax import lax
from jax.experimental import pallas as pl
from jax.experimental.pallas import tpu as pltpu
from jax.sharding import PartitionSpec as P

NORM_EPS = 1e-6
IN_SPECS = (P('dp', 'sp', None), P(), P(), P(), P(None, 'tp', None), P('tp', None), P(None, 'tp', None), P(None, 'tp', None), P('tp', None), P('tp', None, None), P(), P(), P(), P(None, 'tp'), P('tp'), P('tp', None), P(), P('dp', None))
OUT_SPECS = (P('dp', None), P('dp', 'sp', None), P('dp'), P('dp', 'tp', None), P('dp', 'tp', None), P('dp', 'tp', None), P(('dp', 'tp'), None, None), P('dp', 'tp'), P(('dp', 'tp'), None))
F32, BF16 = jnp.float32, jnp.bfloat16
MESH = pl.DeviceIdType.MESH
IMGS, TOK, WIDTH, HD, HEADS, TP, SP = 64, 128, 768, 64, 3, 4, 4
ROWS = IMGS * TOK
HDS = HEADS * HD
GROUP = IMGS // SP
SLOT = 8
PAIRS = TP // 2
SLOTS = PAIRS * SLOT
QUARTER = HDS // 4
SCALE = HD ** -0.5


def dot(a, b, dims):
    return lax.dot_general(a, b, (dims, ((), ())), preferred_element_type=F32)


nn = functools.partial(dot, dims=((1,), (0,)))
nt = functools.partial(dot, dims=((1,), (1,)))
tn = functools.partial(dot, dims=((0,), (0,)))


def hi_lo(a):
    hi = a.astype(BF16).astype(F32)
    return jnp.concatenate([hi, a - hi], axis=0).astype(BF16)


def fold(a):
    half = a.shape[0] // 2
    return a[:half] + a[half:]


def row_mean(a):
    return jnp.mean(a, axis=-1, keepdims=True)


def iota(shape, axis):
    return lax.broadcasted_iota(jnp.int32, shape, axis)


def middle_kernel(x_hbm, gain_1d, bias_1d, probe_1d, wq, wk, wv, wo, bq_ref, bv_ref, bout_1d, hgain_1d, hbias_1d, bup_1d, bdown_1d, wup_hbm, wdown_hbm, og,
                  pooled_o, small_o, xh_o, a_o, z_o, uc_o, coef_o, y_o, hid_o, gpre_o, ga_o, o_o, go_o, hb_o,
                  xin, h0, h1, h2, h3, wup, wdown, u_rx, sg0, sg1, sg2, sg3, eg0, eg1, eg2, eg3, inv_ref, ml, f_ref, w_ref, d_ref, hb, hbrx, hbg, arx, att_all, o_all,
                  gh_ref, gnrx, plrx, pl_all, ga_all, wv_all, go_all, zl, z_ref, a_s, z_s, uc_s, coef_s, y_s, hid_s, gpre_s, ga_s, hb_s, pool_s, small_s, r_acc, rrx, gprx, lsem, ssem, rsem):
    dp, t, s = lax.axis_index('dp'), lax.axis_index('tp'), lax.axis_index('sp')
    s1 = s + 1 - 2 * lax.rem(s, 2)
    s2 = lax.rem(s + 2, 4)
    s3 = lax.rem(s1 + 2, 4)
    sps = (s, s1, s2, s3)
    tps = tuple(lax.rem(t + k, 4) for k in range(4))
    pair, odd = t // 2, lax.rem(t, 2)
    mine = pl.ds(pl.multiple_of(s * GROUP, GROUP), GROUP)
    started = []
    index = iter(range(N_MESSAGES))

    def remote(src, dst, device):
        sem = next(index)
        copy = pltpu.make_async_remote_copy(src_ref=src, dst_ref=dst, send_sem=ssem.at[sem], recv_sem=rsem.at[sem], device_id=device, device_id_type=MESH)
        copy.start()
        started.append(copy)
        return copy

    def to_tp(src, dst):
        return [remote(src, dst, (dp, tps[k], s)) for k in (2, 1, 3)]

    def to_sp(src, dst):
        return [remote(src, dst, (dp, t, sps[d])) for d in (3, 2, 1)]

    def arrive(copies):
        for copy in copies:
            copy.wait_recv()

    puts = []

    def put(src, dst):
        puts.append(pltpu.make_async_copy(src, dst, lsem.at[6 + len(puts)]))
        puts[-1].start()

    def own(rows):
        return jnp.where(odd == 1, pltpu.roll(rows, SLOT // 2, 0), rows)

    order = (3, 2, 1, 0)
    span = GROUP * TOK
    bases = [pl.multiple_of(sps[d] * span, span) for d in order]
    x_copies = [pltpu.make_async_copy(x_hbm.at[pl.ds(base, span)], xin.at[pl.ds(i * span, span)], lsem.at[i]) for i, base in enumerate(bases)]
    normed, raws, exps = (h0, h1, h2, h3), (sg0, sg1, sg2, sg3), (eg0, eg1, eg2, eg3)
    x_copies += [pltpu.make_async_copy(wup_hbm, wup, lsem.at[4]), pltpu.make_async_copy(wdown_hbm, wdown, lsem.at[5])]
    for copy in x_copies:
        copy.start()

    o_all[...] = jnp.zeros_like(o_all)
    go_all[...] = jnp.zeros_like(go_all)
    gprx[...] = jnp.zeros_like(gprx)
    barrier = pltpu.get_barrier_semaphore()
    peers = [(dp, tps[k], sps[d]) for k in range(4) for d in range(4) if (k, d) != (0, 0)]
    peers += [(1 - dp, t, s)]
    for peer in peers:
        pl.semaphore_signal(barrier, inc=1, device_id=peer, device_id_type=MESH)

    gain, bias, probe, bout, hgain, hbias, bup, bdown = [v[...].reshape(1, WIDTH) for v in (gain_1d, bias_1d, probe_1d, bout_1d, hgain_1d, hbias_1d, bup_1d, bdown_1d)]
    bq, bv = [jnp.concatenate([v[h:h + 1] for h in range(HEADS)], axis=1) for v in (bq_ref, bv_ref)]
    probe_rows = jnp.broadcast_to(probe, (16, WIDTH)).astype(BF16)
    query = (nt(probe_rows, wq[...]) + bq).astype(BF16).astype(F32)[:SLOT]
    slot_row, slot_lane = iota((SLOT, HDS), 0), iota((SLOT, HDS), 1) // HD

    def slots_of(parity):
        return (slot_row // 4 == parity) & (lax.rem(slot_row, 4) == slot_lane)

    diag = slots_of(0)
    u_rx[t] = fold(nn(hi_lo(jnp.where(slots_of(odd), query, 0.0)), wk[...]))
    wv_all[t] = wv[...].astype(F32)
    head_shift = fold(nt(hi_lo(jnp.broadcast_to(bias, (SLOT, WIDTH))), wv[...]))[0:1] + bv

    norm_rows = 2 * TOK
    image_lane = iota((TOK, TOK), 1)

    def norm_step(i, n):
        rows = slice(i * norm_rows, (i + 1) * norm_rows)
        x = xin[n * span + i * norm_rows:n * span + (i + 1) * norm_rows].astype(F32)
        centred = x - row_mean(x)
        inv = lax.rsqrt(row_mean(centred * centred) + NORM_EPS)
        normed[n][rows] = (centred * inv).astype(BF16)
        image = n * GROUP + 2 * i
        inv_ref[...] = jnp.where(image_lane == image, inv[:TOK], jnp.where(image_lane == image + 1, inv[TOK:], inv_ref[...]))

    def norm_steps(i, n):
        norm_step(2 * i, n)
        norm_step(2 * i + 1, n)

    def norm_done(n):
        put(normed[n], xh_o.at[pl.ds(bases[n], span)])

    pl.semaphore_wait(barrier, len(peers))
    u_copies = to_tp(u_rx.at[t], u_rx.at[t])
    x_copies[0].wait()
    for i in range(span // norm_rows // 2):
        norm_steps(i, 0)
    norm_done(0)
    quarters = [pl.ds(pl.multiple_of((lax.rem(s, 2) + 2 * x) * QUARTER, 16), QUARTER) for x in (dp, 1 - dp)]

    def relay_x(whole, copies):
        arrive(copies)
        blocks = [whole.at[tps[(4 - k) % 4], quarters[0]] for k in (2, 1, 3)]
        across = [remote(b, b, (1 - dp, t, s)) for b in blocks]
        return across, [remote(b, b, (dp, t, s1)) for b in blocks]

    def relay_core(whole, across):
        arrive(across)
        blocks = [whole.at[tps[(4 - k) % 4], quarters[1]] for k in (2, 1, 3)]
        return [remote(b, b, (dp, t, s1)) for b in blocks]

    arrive(u_copies)
    wv_copies = to_tp(wv_all.at[t, quarters[0]], wv_all.at[t, quarters[0]])
    u = jnp.concatenate([(u_rx[2 * k] + u_rx[2 * k + 1]) * gain for k in range(PAIRS)], axis=0)
    u_split = hi_lo(u)
    uc_s[...] = (u - row_mean(u)).astype(BF16)
    put(uc_s, uc_o)
    lane = iota((SLOTS, TOK), 1)
    wide = 4 * TOK

    def score_step(i, carry, n):
        m_all, l_all = carry
        raw = fold(nt(u_split, normed[n][i * wide:(i + 1) * wide]))
        raws[n][:, :, i * wide:(i + 1) * wide] = raw.reshape(PAIRS, SLOT, wide)
        for j in range(wide // TOK):
            score = raw[:, j * TOK:(j + 1) * TOK] * SCALE
            top = jnp.max(score, axis=1, keepdims=True)
            e = jnp.exp(score - top)
            total = jnp.sum(e, axis=1, keepdims=True)
            exps[n][:, :, i * wide + j * TOK:i * wide + (j + 1) * TOK] = e.reshape(PAIRS, SLOT, TOK)
            here = lane == i * (wide // TOK) + j
            m_all = jnp.where(here, top, m_all)
            l_all = jnp.where(here, total, l_all)
        return m_all, l_all

    def scores(n, ahead):
        carry = (jnp.zeros((SLOTS, TOK), F32), jnp.ones((SLOTS, TOK), F32))
        for i in range(span // wide):
            carry = score_step(i, carry, n)
            if ahead is not None:
                norm_steps(i, ahead)
        return carry

    def sums(n, ahead):
        for i in range(GROUP):
            lanes = slice(i * TOK, (i + 1) * TOK)
            result = fold(nn(hi_lo(own(exps[n][pair, :, lanes])), normed[n][lanes]))
            for h in range(HEADS):
                hb[n, h, i:i + 1, :] = result[h:h + 1]
            if ahead is not None and i % 4 == 3:
                norm_steps(i // 4, ahead)

    ml_copies, hb_copies = [], []
    for n, (d, base) in enumerate(zip(order, bases)):
        ahead = {0: (1, 2), 1: (3, None)}.get(n, (None, None))
        for a in ahead:
            if a is not None:
                x_copies[a].wait()
        m_own, l_own = scores(n, ahead[0])
        ml[s, sps[d], 0:SLOTS] = m_own
        ml[s, sps[d], SLOTS:] = l_own
        ml_copies.append(to_sp(ml.at[s, sps[d]], ml.at[s, sps[d]]))
        sums(n, ahead[1])
        for a in ahead:
            if a is not None:
                norm_done(a)
        if d:
            hb_copies.append(remote(hb.at[n], hbrx.at[s], (dp, t, sps[d])))
        else:
            hbrx[s] = hb[n]

    def weights_of(g, sources):
        tops = [ml[k, g, 0:SLOTS] for k in range(SP)]
        top = functools.reduce(jnp.maximum, tops)
        total = sum(ml[k, g, SLOTS:] * jnp.exp(tops[k] - top) for k in range(SP))
        return [jnp.exp(ml[k, g, 0:SLOTS] - top) / total for k in sources]

    for i, d in enumerate((3, 2, 1)):
        ml_copies[i][i].wait_recv()
    cols = []
    for k, weight in enumerate(weights_of(s, range(SP))):
        w_ref[k] = weight.reshape(PAIRS, SLOT, TOK)
        cols.append(own(w_ref[k, pair]).T)
    arrive(hb_copies)
    lane_head = iota((GROUP, HDS), 1) // HD
    o_part = jnp.zeros((GROUP, HDS), F32)
    for h in range(HEADS):
        hsum = sum(hbrx[k, h] * cols[k][0:GROUP, h:h + 1] for k in range(SP)) * gain
        hbg[h, mine, :] = hsum + bias
        o_part = jnp.where(lane_head == h, fold(nt(hi_lo(hsum), wv[...])), o_part)
    o_all[mine, 0:HDS] = o_part + head_shift
    arx[t] = nn((o_part + head_shift).astype(BF16), wo[...])
    att_copies = to_tp(arx.at[t], arx.at[t])
    hbg_copies = to_sp(hbg.at[:, mine], hbg.at[:, mine])
    wv_across, wv_core = relay_x(wv_all, wv_copies)
    x_copies[4].wait()
    x_copies[5].wait()
    grad_hidden = nt(og[...], wdown[...])
    gh_ref[...] = grad_hidden
    for i, d in enumerate((3, 2, 1)):
        arrive([c for j, c in enumerate(ml_copies[i]) if j != i])
    arrive(ml_copies[3])
    for g in range(SP):
        f_ref[g] = weights_of(sps[3 - g], [s])[0]
    inv_ref[...] = inv_ref[...].T
    arrive(att_copies)
    att16 = arx[0] + arx[1] + arx[2] + arx[3] + bout
    att_all[mine, :] = att16

    def mlp(att, grad_hidden):
        centred = att - row_mean(att)
        inv = lax.rsqrt(row_mean(centred * centred) + NORM_EPS)
        unit = centred * inv
        y = (unit * hgain + hbias).astype(BF16)
        pre = nn(y, wup[...]) + bup
        square = pre * pre
        tanh = jnp.tanh((2 / jnp.pi) ** 0.5 * (pre + 0.044715 * (square * pre)))
        slope = 0.5 * (1.0 + tanh) + 0.5 * pre * (1.0 - tanh * tanh) * ((2 / jnp.pi) ** 0.5 * (1.0 + 3 * 0.044715 * square))
        gpre = (grad_hidden * slope).astype(BF16)
        hid = (0.5 * pre * (1.0 + tanh)).astype(BF16)
        return inv, unit, y, gpre, hid

    inv, unit, _, gpre, hid = mlp(att16, gh_ref[mine, :])
    gnrx[t] = nt(gpre, wup[...])
    gn_copies = to_tp(gnrx.at[t], gnrx.at[t])
    att_copies = to_sp(att_all.at[mine], att_all.at[mine])
    o_copies = to_sp(o_all.at[mine], o_all.at[mine])
    plrx[t] = nn(hid, wdown[...])
    arrive(gn_copies)
    grad_y = (gnrx[0] + gnrx[1] + gnrx[2] + gnrx[3]) * hgain
    grad_att = og[mine, :].astype(F32) + inv * (grad_y - row_mean(grad_y) - unit * row_mean(grad_y * unit))
    go = nt(grad_att.astype(BF16), wo[...]).astype(BF16).astype(F32)
    tail_lane = iota((GROUP, HD), 1)
    tail = jnp.zeros((GROUP, HD), F32)
    for h in range(HEADS):
        delta = jnp.sum(jnp.where(lane_head == h, go * o_part, 0.0), axis=1, keepdims=True)
        tail = jnp.where(tail_lane == h, delta, tail)
    go_all[t, mine, 0:HDS] = go
    go_all[t, mine, HDS:] = tail
    go_copies = to_tp(go_all.at[t, mine], go_all.at[t, mine])
    ga_all[mine, :] = grad_att
    ga_copies = to_sp(ga_all.at[mine], ga_all.at[mine])
    wv_second = relay_core(wv_all, wv_across)
    arrive(att_copies)
    _, _, y, gpre, hid = mlp(att_all[...], gh_ref[...])
    for value, kept, out in ((y, y_s, y_o), (gpre, gpre_s, gpre_o), (hid, hid_s, hid_o)):
        kept[...] = value
        put(kept, out)
    arrive(wv_core)
    arrive(wv_second)
    arrive(go_copies)
    go_copies = to_sp(go_all.at[:, mine], go_all.at[:, mine])
    pl_copies = to_tp(plrx.at[t], plrx.at[t])

    def z_group(g, n):
        block = [go_all[k, pl.ds(pl.multiple_of(g * GROUP, GROUP), GROUP)] for k in range(TP)]
        for j in range(PAIRS):
            deltas = [jnp.concatenate([block[2 * j + k][:, TOK:], jnp.zeros((TOK - GROUP, TOK), F32)], axis=0).T[HD:HD + SLOT // 2] for k in range(2)]
            d_ref[n, j] = jnp.concatenate(deltas, axis=0)
        for k in range(TP):
            mask = jnp.where(slots_of(k % 2), 1.0, 0.0)
            for i in range(GROUP):
                zl[n, k, i * SLOT:(i + 1) * SLOT, :] = block[k][i:i + 1, 0:HDS] * mask
        for j in range(PAIRS):
            z_ref[n, j] = sum(nn(zl[n, 2 * j + k].astype(BF16), wv_all[2 * j + k].astype(BF16)) for k in range(2)) * gain

    r_acc[...] = jnp.zeros_like(r_acc)
    batch = 4

    def back_step(i, g, n):
        x = normed[n][i * batch * TOK:(i + 1) * batch * TOK]
        grads = []
        for j in range(batch):
            image = i * batch + j
            z = jnp.concatenate([z_ref[n, k, image * SLOT:(image + 1) * SLOT] for k in range(PAIRS)], axis=0)
            grads.append(fold(nt(hi_lo(z), x[j * TOK:(j + 1) * TOK])))
            z_s[n * GROUP + image] = (z - row_mean(z)).astype(BF16)
        all_ds = []
        for j, grad_p in enumerate(grads):
            image = i * batch + j
            lanes = slice(image * TOK, (image + 1) * TOK)
            f_col = f_ref[n][:, image:image + 1]
            d_col = d_ref[n].reshape(SLOTS, TOK)[:, image:image + 1]
            p = exps[n][:, :, lanes].reshape(SLOTS, TOK) * f_col
            ds = p * (grad_p - d_col) * SCALE
            raw = raws[n][:, :, lanes].reshape(SLOTS, TOK)
            row = n * GROUP + image
            inv_row = inv_ref[row:row + 1, :]
            coef_s[row:row + 1, :] = jnp.sum(ds * raw + p * grad_p, axis=0, keepdims=True) * inv_row * (-1.0 / WIDTH)
            a_s[row] = (jnp.concatenate([ds, p], axis=0) * inv_row).astype(BF16)
            all_ds.append(own(jnp.where(pair == 1, ds[SLOT:], ds[:SLOT])))
        return nn(hi_lo(jnp.concatenate(all_ds, axis=1)), x)

    steps = (0, 1, 3, 2)
    z_group(sps[0], 3)
    for turn, d in enumerate(steps):
        g, n = sps[d], 3 - d
        r_acc[...] += sum(back_step(i, g, n) for i in range(GROUP // batch))
        if d == 0:
            arrive(go_copies)
            arrive(pl_copies)
            pl_all[mine, :] = plrx[0] + plrx[1] + plrx[2] + plrx[3] + att16 + bdown
            pl_copies = to_sp(pl_all.at[mine], pl_all.at[mine])
        if turn < 3:
            z_group(sps[steps[turn + 1]], 3 - steps[turn + 1])
        group, kept = pl.ds(pl.multiple_of(g * GROUP, GROUP), GROUP), pl.ds(n * GROUP, GROUP)
        put(a_s.at[kept], a_o.at[group])
        put(z_s.at[kept], z_o.at[group])
        put(coef_s.at[kept], coef_o.at[group])
    arrive(o_copies)
    put(o_all, o_o)
    put(go_all.at[t], go_o)

    r_part = fold(r_acc[...]) * gain
    rrx[s] = r_part
    r_copies = to_sp(rrx.at[s], rrx.at[s])

    def query_grad(r_rows):
        return jnp.sum(jnp.where(diag, fold(nt(hi_lo(r_rows), wk[...])), 0.0), axis=0, keepdims=True)

    gq_part = jnp.where(iota((SLOT, HDS), 0) == 0, query_grad(r_part), 0.0)
    gp_part = fold(nn(hi_lo(gq_part), wq[...]))
    slot = t * SP + s
    for i in range(WIDTH // TOK):
        gprx[slot, i:i + 1, :] = gp_part[0:1, i * TOK:(i + 1) * TOK]
    gp_copies = [remote(gprx.at[slot], gprx.at[slot], (dp, tps[k], sps[d])) for k in (2, 1, 3, 0) for d in (3, 2, 1, 0) if (k, d) != (0, 0)]

    arrive(pl_copies)
    pool_s[...] = pl_all[...].astype(BF16)
    put(pool_s, pooled_o)
    arrive(ga_copies)
    ga_s[...] = ga_all[...].astype(BF16)
    put(ga_s, ga_o)
    arrive(hbg_copies)
    hb_s[...] = hbg[...].astype(BF16)
    put(hb_s, hb_o)
    arrive(r_copies)
    r_sum = rrx[0] + rrx[1] + rrx[2] + rrx[3]
    small_s[...] = r_sum
    small_s[3:4, :] = jnp.zeros((1, WIDTH), F32)
    small_s[4:5, :] = jnp.zeros((1, WIDTH), F32)
    small_s[3:4, 0:HDS] = query_grad(r_sum)
    small_s[4:5, 0:HDS] = query[0:1]
    arrive(gp_copies)
    gp = sum(gprx[i] for i in range(TP * SP))
    for i in range(WIDTH // TOK):
        small_s[5:6, i * TOK:(i + 1) * TOK] = gp[i:i + 1]
    put(small_s, small_o)
    for copy in started:
        copy.wait_send()
    for copy in puts:
        copy.wait()


N_MESSAGES = 112


def middle(*args):
    vm, sds = pltpu.VMEM, jax.ShapeDtypeStruct
    wide = sds((IMGS, WIDTH), BF16)
    outs = (wide, sds((SLOT, WIDTH), F32), sds((ROWS, WIDTH), BF16), sds((IMGS, 2 * SLOTS, TOK), BF16), sds((IMGS, SLOTS, WIDTH), BF16), sds((SLOTS, WIDTH), BF16), sds((IMGS, TOK), F32),
            wide, wide, wide, wide, sds((IMGS, 256), F32), sds((IMGS, 256), F32), sds((HEADS, IMGS, WIDTH), BF16))
    scratch = [vm((ROWS, WIDTH), BF16)] + [vm((GROUP * TOK, WIDTH), BF16)] * 4 + [vm((WIDTH, WIDTH), BF16), vm((WIDTH, WIDTH), BF16), vm((TP, SLOT, WIDTH), F32),
               *([vm((PAIRS, SLOT, GROUP * TOK), F32)] * 8), vm((TOK, TOK), F32), vm((SP, SP, 2 * SLOTS, TOK), F32), vm((SP, SLOTS, TOK), F32), vm((SP, PAIRS, SLOT, TOK), F32), vm((SP, PAIRS, SLOT, TOK), F32),
               vm((SP, HEADS, GROUP, WIDTH), F32), vm((SP, HEADS, GROUP, WIDTH), F32), vm((HEADS, IMGS, WIDTH), F32),
               vm((TP, GROUP, WIDTH), F32), vm((IMGS, WIDTH), F32), vm((IMGS, 256), F32),
               vm((IMGS, WIDTH), F32), vm((TP, GROUP, WIDTH), F32), vm((TP, GROUP, WIDTH), F32), vm((IMGS, WIDTH), F32),
               vm((IMGS, WIDTH), F32), vm((TP, HDS, WIDTH), F32), vm((TP, IMGS, 256), F32), vm((SP, TP, GROUP * SLOT, HDS), F32), vm((SP, PAIRS, GROUP * SLOT, WIDTH), F32),
               vm((IMGS, 2 * SLOTS, TOK), BF16), vm((IMGS, SLOTS, WIDTH), BF16), vm((SLOTS, WIDTH), BF16), vm((IMGS, TOK), F32),
               vm((IMGS, WIDTH), BF16), vm((IMGS, WIDTH), BF16), vm((IMGS, WIDTH), BF16), vm((IMGS, WIDTH), BF16), vm((HEADS, IMGS, WIDTH), BF16), vm((IMGS, WIDTH), BF16), vm((SLOT, WIDTH), F32), vm((2 * SLOT, WIDTH), F32),
               vm((SP, SLOT, WIDTH), F32), vm((TP * SP, SLOT, TOK), F32),
               pltpu.SemaphoreType.DMA((32,)), pltpu.SemaphoreType.DMA((N_MESSAGES,)), pltpu.SemaphoreType.DMA((N_MESSAGES,))]
    any_spec, vm_spec = pl.BlockSpec(memory_space=pl.ANY), pl.BlockSpec(memory_space=vm)
    in_specs = [any_spec] + [vm_spec] * 14 + [any_spec] * 2 + [vm_spec]
    out_specs = [any_spec] * len(outs)
    return pl.pallas_call(middle_kernel, out_shape=outs, in_specs=in_specs, out_specs=out_specs, scratch_shapes=scratch,
                          compiler_params=pltpu.CompilerParams(collective_id=0, has_side_effects=True, vmem_limit_bytes=63 * 1024 * 1024), name='middle')(*args)


CHUNKS = 16
AHEAD = 5


def final_kernel(xh, a, z, uc, coef, y, gpre, hid, og, o, ga, go, hb, small, probe, pool,
                 gx, gup, gdown, gout, gvalue, gquery, gkey, gprobe, pooled,
                 x_v, gx_v, a_v, z_v, coef_v, uc_v, small_v, pool_v, y_v, gpre_v, hid_v, og_v, o_v, ga_v, go_v, hb_v, gup_v, gdown_v, gout_v, gvalue_v, gquery_v, gkey_v, in_sem, x_sem, az_sem, out_sem, gx_sem):
    images = IMGS // CHUNKS
    rows = images * TOK
    parts = 4

    def block(ref, i, size):
        return ref.at[pl.ds(pl.multiple_of(i * size, size), size)]

    def x_in(i):
        return pltpu.make_async_copy(block(xh, i, rows), block(x_v, i, rows), x_sem.at[i])

    def gx_out(i):
        return pltpu.make_async_copy(block(gx_v, i, rows), block(gx, i, rows), gx_sem.at[i])

    az = [pltpu.make_async_copy(block(src, i, IMGS // parts), block(dst, i, IMGS // parts), az_sem.at[2 * i + n]) for i in range(parts) for n, (src, dst) in enumerate(((a, a_v), (z, z_v)))]
    pairs = ((coef, coef_v), (uc, uc_v), (small, small_v), (pool, pool_v), (y, y_v), (gpre, gpre_v), (hid, hid_v), (og, og_v), (o, o_v), (ga, ga_v), (go, go_v), (hb, hb_v))
    ins = [pltpu.make_async_copy(src, dst, in_sem.at[n]) for n, (src, dst) in enumerate(pairs)]
    for copy in ins[:2] + az[:2]:
        copy.start()
    x_in(0).start()
    x_in(1).start()
    for copy in ins[2:] + az[2:]:
        copy.start()
    for c in range(2, AHEAD):
        x_in(c).start()
    outs = []

    def put(src, dst):
        outs.append(pltpu.make_async_copy(src, dst, out_sem.at[len(outs)]))
        outs[-1].start()

    ins[0].wait()
    ins[1].wait()
    cols = jnp.concatenate([coef_v[...]] * (TOK // IMGS), axis=0).T
    col_lane = iota((TOK, TOK), 1)

    def chunk_step(c):
        x_in(c).wait()
        for j in range(images):
            b = c * images + j
            start = pl.ds(pl.multiple_of(b * TOK, TOK), TOK)
            mixed = tn(a_v[b], jnp.concatenate([uc_v[...], z_v[b]], axis=0))
            col = jnp.sum(jnp.where(col_lane == b, cols, 0.0), axis=1, keepdims=True)
            gx_v[start] = (mixed + x_v[start].astype(F32) * col).astype(BF16)
        gx_out(c).start()

        @pl.when(c + AHEAD < CHUNKS)
        def _():
            x_in(c + AHEAD).start()

    for part in range(parts):
        az[2 * part].wait()
        az[2 * part + 1].wait()
        pl.loop(part * CHUNKS // parts, (part + 1) * CHUNKS // parts)(chunk_step)
        if part == 0:
            for copy in ins[2:]:
                copy.wait()
            turned = jnp.concatenate([small_v[...], jnp.zeros((TOK - SLOT, WIDTH), F32)], axis=0)[:, :256].T
            gquery_v[...] = turned[:HDS, 3:4] * probe[...].reshape(1, WIDTH)
            put(gquery_v, gquery)
            for h in range(HEADS):
                gkey_v[h * HD:(h + 1) * HD] = turned[h * HD:(h + 1) * HD, 4:5] * small_v[h:h + 1]
            put(gkey_v, gkey)
            gprobe[...] = small_v[5]
            put(pool_v, pooled)
            gup_v[...] = tn(y_v[...], gpre_v[...])
            put(gup_v, gup)
        if part == 1:
            gdown_v[...] = tn(hid_v[...], og_v[...])
            put(gdown_v, gdown)
        if part == 2:
            gout_v[...] = tn(o_v[...].astype(BF16), ga_v[...])[:HDS]
            put(gout_v, gout)
            for h in range(HEADS):
                gvalue_v[h * HD:(h + 1) * HD] = tn(go_v[...].astype(BF16), hb_v[h])[h * HD:(h + 1) * HD]
            put(gvalue_v, gvalue)
    for copy in outs:
        copy.wait()

    @pl.loop(0, CHUNKS)
    def _(c):
        gx_out(c).wait()


def final(*args):
    sds, vm = jax.ShapeDtypeStruct, pltpu.VMEM
    outs = (sds((ROWS, WIDTH), BF16), sds((WIDTH, WIDTH), F32), sds((WIDTH, WIDTH), F32)) + (sds((HDS, WIDTH), F32),) * 4 + (sds((WIDTH,), F32), sds((IMGS, WIDTH), BF16))
    any_spec, vm_spec = pl.BlockSpec(memory_space=pl.ANY), pl.BlockSpec(memory_space=vm)
    in_specs = [any_spec] * 14 + [vm_spec, any_spec]
    wide = vm((IMGS, WIDTH), BF16)
    scratch = [vm((ROWS, WIDTH), BF16), vm((ROWS, WIDTH), BF16), vm((IMGS, 2 * SLOTS, TOK), BF16), vm((IMGS, SLOTS, WIDTH), BF16),
               vm((IMGS, TOK), F32), vm((SLOTS, WIDTH), BF16), vm((SLOT, WIDTH), F32), wide, wide, wide, wide, wide, vm((IMGS, 256), F32), wide, vm((IMGS, 256), F32), vm((HEADS, IMGS, WIDTH), BF16),
               vm((WIDTH, WIDTH), F32), vm((WIDTH, WIDTH), F32)] + [vm((HDS, WIDTH), F32)] * 4
    scratch += [pltpu.SemaphoreType.DMA((n,)) for n in (12, CHUNKS, 8, 7, CHUNKS)]
    return pl.pallas_call(final_kernel, out_shape=outs, in_specs=in_specs, out_specs=[any_spec] * 7 + [vm_spec, any_spec], scratch_shapes=scratch,
                          compiler_params=pltpu.CompilerParams(vmem_limit_bytes=63 * 1024 * 1024), name='final')(*args)


def local_head(encoded, enc_gain, enc_bias, probe, w_query, b_query, w_key, w_value, b_value, w_out, b_out, head_gain, head_bias, w_up, b_up, w_down, b_down, out_grad):
    def flat(w):
        return jnp.transpose(w, (1, 2, 0)).reshape(HDS, WIDTH)

    def unflat(g):
        return jnp.transpose(g.reshape(HEADS, HD, WIDTH), (2, 0, 1))

    x = encoded.reshape(ROWS, WIDTH)
    pool, small, xh, a, z, uc, coef, y, hid, gpre, ga, o, go, hb = middle(
        x, enc_gain, enc_bias, probe, flat(w_query), flat(w_key), flat(w_value), w_out.reshape(HDS, WIDTH), b_query, b_value,
        b_out, head_gain, head_bias, b_up, b_down, w_up, w_down, out_grad)
    grad_x, grad_w_up, grad_w_down, grad_w_out, grad_w_value, grad_w_query, grad_w_key, grad_probe, pooled = final(
        xh, a, z, uc, coef, y, gpre, hid, out_grad, o, ga, go, hb, small, probe, pool)
    return (pooled, grad_x.reshape(IMGS, TOK, WIDTH), grad_probe, unflat(grad_w_query), unflat(grad_w_key), unflat(grad_w_value),
            grad_w_out.reshape(HEADS, HD, WIDTH), grad_w_up, grad_w_down)


def solution(mesh):
    return jax.shard_map(local_head, mesh=mesh, in_specs=IN_SPECS, out_specs=OUT_SPECS, check_vma=False)
```

time: 91.6 us -> 74.9 us (0.82)
  Pallas kernels: 90.7 us -> 73.8 us
    pallas_call x1, Pallas kernels: 73.3 us -> 59.2 us  [middle(): pl.pallas_call(middle_kernel, out_shape=outs, in_specs=in_specs, out_spec...]
    pallas_call x1, Pallas kernels: 17.4 us -> 14.7 us  [final(): pl.pallas_call(final_kernel, out_shape=outs, in_specs=in_specs, out_specs...]
where the time goes in v3:
time: 74.9 us; the launch traced here: 74.7 us
  Pallas kernels  73.8 us (99%)
  between operations  0.82 us (1%)
    pallas_call x1, Pallas kernels, middle(): pl.pallas_call(middle_kernel, out_shape=outs, in_specs=in_specs, out_spec...  59.2 us
    pallas_call x1, Pallas kernels, final(): pl.pallas_call(final_kernel, out_shape=outs, in_specs=in_specs, out_specs...  14.7 us

profile of v3, /device:TPU:0, one launch (start us, length us, event | category | flops | bytes accessed | tf_op | source)
XLA Modules:
  0.0 74.7 jit_solution(2121880523484109793)
XLA Ops:
  0.6 59.2 %middle.1 = (bf16[64,768]{1,0:T(8,128)(2,1)}, f32[8,768]{1,0:T(8,128)}, bf16[8192,768]{1,0:T(8,128)(2,1)}, bf16[64,32,128]{2,1,0:T(8,128)(2,1)}, bf16[64,16,768]...) custom-call(bf16[8192,768]{1,0:T(8,128)(2,1)} %bitcast.22, ...), custom_call_target="tpu_custom_call" | custom-call | tf_op jit(solution)/shard_map/middle/pallas_call | solution.py:427
  59.8 14.7 %final.1 = (bf16[8192,768]{1,0:T(8,128)(2,1)}, f32[768,768]{1,0:T(8,128)}, f32[768,768]{1,0:T(8,128)}, f32[192,768]{1,0:T(8,128)}, f32[192,768]{1,0:T(8,128)}, /...) custom-call(bf16[8192,768]{1,0:T(8,128)(2,1)} %get-tuple-element.32.xh, ...), custom_call_target="tpu_custom_call" | custom-call | tf_op jit(solution)/shard_map/final/pallas_call | solution.py:531
